TPU v7x, 128 devices: a whole 4x4x4 slice. The times are simulated.
128 devices in a mesh: seq: 128 (over y, z, x, core).
Axes of the slice: x: 4, y: 4, z: 4, core: 2. Of those that a mesh axis runs over, the one named last changes fastest.
Arguments:
- residual: bfloat16 [16384, 2560], P('seq'), may hold values from -6 to 6
- queries: bfloat16 [16384, 2560], P('seq'), may hold values from -5 to 5, as said below
- keys: bfloat16 [16384, 512], P('seq'), may hold values from -5 to 5
- values: bfloat16 [16384, 512], P('seq'), may hold values from -6 to 6
- out_proj: bfloat16 [2560, 2560], P(None, 'seq'), may hold values from -0.125 to 0.125
- norm_gain: float32 [2560], replicated, may hold values from 0.25 to 1.75
- expert_in: bfloat16 [2560, 2, 106496], P(None, None, 'seq'), may hold values from -0.125 to 0.125
- expert_down: bfloat16 [106496, 2560], P('seq'), may hold values from -0.15625 to 0.15625
- routes: int32 [16384, 2], P('seq'), may hold values from 0 to 63, all different within a row
- gate_ints: int32 [16384, 2], P('seq'), may hold values from 1 to 1023
- modality: int32 [16384], P('seq'), may hold values 0 or 1
- capacity: int32 [64, 2], replicated, may hold values from 1 to 2, as said below
Outputs:
- attended: bfloat16 [16384, 2560], P('seq')
- expert_mix: bfloat16 [16384, 2560], P('seq')
Inputs may be any that keep to these rules, and one draw needn't show every extreme that they name: `queries` and `keys`: every element lies between -5 and 5. `routes`: each token names two different experts. `capacity`: some entry equals 2.
All inputs are finite; a program needn't handle non-finite values. No bound on the sum of `modality` on one device may be relied on, other than what follows from the above.
Results may differ from a plain program's by a relative error of at most 0.0086.
Values may be sent and summed in bfloat16 or wider, within the bound.
A program may use at most 192 MiB of HBM per device.

v0:
```python
import jax
import jax.numpy as jnp
from jax import lax
from jax.sharding import PartitionSpec as P

HEADS = 20
KV_HEADS = 4
HEAD = 128
WINDOW = 1024
EXPERTS = 64
CAP = 2


def shifted(value, axis, steps):
    count = lax.axis_size(axis)
    initial, last = (max(0, -steps), min(count, count - steps))
    return lax.ppermute(value, axis, [(source, source + steps) for source in range(initial, last)])


def swapped(value, axis, distance):
    mask = 2**distance
    pairs = [(source, source ^ mask) for source in range(lax.axis_size(axis))]
    return lax.ppermute(value, axis, pairs)


def body(
    residual,
    queries,
    keys,
    values,
    out_proj,
    norm_gain,
    expert_in,
    expert_down,
    routes,
    gate_ints,
    modality,
    capacity,
):
    devices = lax.axis_size("seq")
    device_pos = lax.axis_index("seq")
    tok_rows = residual.shape[0]
    width_d = residual.shape[1]
    q_group = HEADS // KV_HEADS
    blocks_back = (WINDOW + tok_rows - 1) // tok_rows
    earlier = []
    moving = (keys, values)
    for step_back in range(blocks_back):
        moving = shifted((moving[0], moving[1]), "seq", 1)
        earlier.insert(0, moving)
    all_keys = jnp.concatenate([pair_kv[0] for pair_kv in earlier] + [keys], 0)
    all_values = jnp.concatenate([pair_kv[1] for pair_kv in earlier] + [values], 0)
    key_span = all_keys.shape[0]
    q_pos = device_pos * tok_rows + jnp.arange(tok_rows, dtype=jnp.int32)
    k_pos = (device_pos - blocks_back) * tok_rows + jnp.arange(key_span, dtype=jnp.int32)
    visible = (
        (k_pos[None, :] <= q_pos[:, None])
        & (k_pos[None, :] > q_pos[:, None] - WINDOW)
        & (k_pos[None, :] >= 0)
    )
    score_scale = HEAD ** (-0.5)
    query_heads = jnp.transpose(queries.reshape(tok_rows, KV_HEADS, q_group, HEAD), (1, 0, 2, 3))
    key_heads = jnp.transpose(all_keys.reshape(key_span, KV_HEADS, HEAD), (1, 0, 2))
    value_heads = jnp.transpose(all_values.reshape(key_span, KV_HEADS, HEAD), (1, 0, 2))

    def one_head(operands):
        q_one, k_one, v_one = operands
        scores = (
            jnp.einsum("qgd,kd->gqk", q_one, k_one, preferred_element_type=jnp.float32)
            * score_scale
        )
        scores = jnp.where(visible[None], scores, -jnp.inf)
        row_max = jnp.max(scores, -1, keepdims=True)
        weights_raw = jnp.exp(scores - row_max)
        probs_bf = (weights_raw / jnp.sum(weights_raw, -1, keepdims=True)).astype(jnp.bfloat16)
        return jnp.einsum(
            "gqk,kd->qgd", probs_bf, v_one, preferred_element_type=jnp.float32
        ).astype(jnp.bfloat16)

    context = lax.map(one_head, (query_heads, key_heads, value_heads))
    context = jnp.transpose(context, (1, 0, 2, 3)).reshape(tok_rows, HEADS * HEAD)
    whole_proj = lax.all_gather(out_proj, "seq", axis=1, tiled=True)
    attended = jnp.dot(context, whole_proj, preferred_element_type=jnp.float32).astype(jnp.bfloat16)
    attended = lax.optimization_barrier(attended)
    hidden = residual.astype(jnp.float32) + attended.astype(jnp.float32)
    normed = (
        hidden * lax.rsqrt(jnp.mean(hidden * hidden, -1, keepdims=True) + 1e-05) * norm_gain
    ).astype(jnp.bfloat16)
    slot_count = 2 * CAP
    local_experts = max(1, EXPERTS // devices)
    chosen = routes.reshape(-1)
    modal_flag = jnp.repeat(modality, 2)
    slot_key = chosen * 2 + modal_flag
    onehot = (slot_key[:, None] == jnp.arange(2 * EXPERTS, dtype=jnp.int32)[None, :]).astype(
        jnp.int32
    )
    rank_in = jnp.sum((jnp.cumsum(onehot, 0) - onehot) * onehot, 1)
    limit_of = jnp.sum(onehot * capacity.reshape(1, -1), 1)
    kept_mask = rank_in < limit_of
    column = chosen * slot_count + modal_flag * CAP + rank_in
    select = (
        (column[:, None] == jnp.arange(EXPERTS * slot_count, dtype=jnp.int32)[None, :])
        & kept_mask[:, None]
    ).astype(jnp.bfloat16)
    doubled = jnp.repeat(normed, 2, axis=0)
    slot_table = lax.dot_general(
        select, doubled, (((0,), (0,)), ((), ())), preferred_element_type=jnp.float32
    ).astype(jnp.bfloat16)
    slab_cols = expert_in.shape[2]
    hidden_each = slab_cols // local_experts
    weights_in = expert_in.reshape(width_d, 2, local_experts, hidden_each)
    weights_down = expert_down.reshape(local_experts, hidden_each, width_d)
    outgoing = slot_table.reshape(devices, CAP, width_d)
    own_rows = lax.all_to_all(outgoing, "seq", split_axis=0, concat_axis=0, tiled=True)
    partner = swapped(own_rows, "seq", 0)
    is_lower = device_pos % 2 == 0
    first_half = jnp.where(is_lower, own_rows, partner)
    second_half = jnp.where(is_lower, partner, own_rows)
    rows_in = jnp.stack([first_half, second_half], 1).reshape(devices, 1, slot_count, width_d)
    gate_up = jnp.einsum(
        "nlkd,dglf->glnkf", rows_in, weights_in, preferred_element_type=jnp.float32
    )
    active = (jax.nn.silu(gate_up[0]) * gate_up[1]).astype(jnp.bfloat16)
    partial_value = jnp.einsum(
        "lnkf,lfd->nlkd", active, weights_down, preferred_element_type=jnp.float32
    )
    partial_value = lax.optimization_barrier(partial_value.astype(jnp.bfloat16)).reshape(
        devices, 2, CAP, width_d
    )
    keep_own = jnp.where(is_lower, partial_value[:, 0], partial_value[:, 1])
    give_back = jnp.where(is_lower, partial_value[:, 1], partial_value[:, 0])
    taken = swapped(give_back, "seq", 0)
    summed = (keep_own.astype(jnp.float32) + taken.astype(jnp.float32)).astype(jnp.bfloat16)
    returned = lax.all_to_all(summed, "seq", split_axis=0, concat_axis=0, tiled=True)
    mixed = returned.reshape(EXPERTS * slot_count, width_d)
    gathered_rows = jnp.dot(select, mixed, preferred_element_type=jnp.float32).reshape(
        tok_rows, 2, width_d
    )
    gate_scale = jnp.where(
        kept_mask, gate_ints.reshape(-1).astype(jnp.float32) / 1024.0, 0.0
    ).reshape(tok_rows, 2, 1)
    expert_mix = jnp.sum(gate_scale * gathered_rows, 1).astype(jnp.bfloat16)
    return (attended, expert_mix)


def solution(mesh):
    placed = (
        P("seq", None),
        P("seq", None),
        P("seq", None),
        P("seq", None),
        P(None, "seq"),
        P(),
        P(None, None, "seq"),
        P("seq", None),
        P("seq", None),
        P("seq", None),
        P("seq"),
        P(),
    )
    return jax.shard_map(
        body,
        mesh=mesh,
        in_specs=placed,
        out_specs=(P("seq", None), P("seq", None)),
        check_vma=False,
    )
```

profile of v0, /device:TPU:1, one launch (start us, length us, event | category | flops | bytes accessed | tf_op | source)
XLA Modules:
  0.0 258.9 jit_solution(13102861345022883946)
XLA Ops:
  7.9 4.5 %collective-permute-start = (bf16[128,512]{1,0:T(8,128)(2,1)}, bf16[128,512]{1,0:T(8,128)(2,1)S(1)}, u32[]{:S(2)}, u32[]{:S(2)}) collective-permute-start(bf16[128,512]{1,0:T(8,128)(2,1)} %param.17), channel_id=1, source_target_pairs={{0,1},{1,2},{2,3},{3,4},{4,5},{5,6},{6,7},{7,8},{8,9},{9,10},{10,1... | collective-permute-start | bytes 393224 | tf_op jit(solution)/shard_map/ppermute | solution.py:17
  12.4 1.0 copy.86
  13.5 1.9 collective-permute-start.8
  16.1 3.5 %collective-permute-start.1 = (bf16[128,512]{1,0:T(8,128)(2,1)S(1)}, bf16[128,512]{1,0:T(8,128)(2,1)S(1)}, u32[]{:S(2)}, u32[]{:S(2)}) collective-permute-start(bf16[128,512]{1,0:T(8,128)(2,1)S(1)} %collective-permute-done), channel_id=1, source_target_pairs={{0,1},{1,2},{2,3},{3,4},{4,5},{5,6},{6,7},{7,8},{8,9},{9,10},{10,1... | collective-permute-start | bytes 393224 | tf_op jit(solution)/shard_map/ppermute | solution.py:17
  20.9 1.9 collective-permute-start.9
  22.9 3.2 %collective-permute-start.2 = (bf16[128,512]{1,0:T(8,128)(2,1)S(1)}, bf16[128,512]{1,0:T(8,128)(2,1)S(1)}, u32[]{:S(2)}, u32[]{:S(2)}) collective-permute-start(bf16[128,512]{1,0:T(8,128)(2,1)S(1)} %collective-permute-done.1), channel_id=1, source_target_pairs={{0,1},{1,2},{2,3},{3,4},{4,5},{5,6},{6,7},{7,8},{8,9},{9,10},{10,1... | collective-permute-start | bytes 393224 | tf_op jit(solution)/shard_map/ppermute | solution.py:17
  26.3 2.8 %collective-permute-start.10 = (bf16[128,512]{0,1:T(8,128)(2,1)S(1)}, bf16[128,512]{0,1:T(8,128)(2,1)S(1)}, u32[]{:S(2)}, u32[]{:S(2)}) collective-permute-start(bf16[128,512]{0,1:T(8,128)(2,1)S(1)} %collective-permute-done.9), channel_id=1, source_target_pairs={{0,1},{1,2},{2,3},{3,4},{4,5},{5,6},{6,7},{7,8},{8,9},{9,10},{10,1... | collective-permute-start | bytes 393224 | tf_op jit(solution)/shard_map/ppermute | solution.py:17
  29.2 3.2 %collective-permute-start.3 = (bf16[128,512]{1,0:T(8,128)(2,1)S(1)}, bf16[128,512]{1,0:T(8,128)(2,1)S(1)}, u32[]{:S(2)}, u32[]{:S(2)}) collective-permute-start(bf16[128,512]{1,0:T(8,128)(2,1)S(1)} %collective-permute-done.2), channel_id=1, source_target_pairs={{0,1},{1,2},{2,3},{3,4},{4,5},{5,6},{6,7},{7,8},{8,9},{9,10},{10,1... | collective-permute-start | bytes 393224 | tf_op jit(solution)/shard_map/ppermute | solution.py:17
  32.4 3.3 %collective-permute-start.11 = (bf16[128,512]{0,1:T(8,128)(2,1)S(1)}, bf16[128,512]{0,1:T(8,128)(2,1)S(1)}, u32[]{:S(2)}, u32[]{:S(2)}) collective-permute-start(bf16[128,512]{0,1:T(8,128)(2,1)S(1)} %collective-permute-done.10), channel_id=1, source_target_pairs={{0,1},{1,2},{2,3},{3,4},{4,5},{5,6},{6,7},{7,8},{8,9},{9,10},{10,1... | collective-permute-start | bytes 393224 | tf_op jit(solution)/shard_map/ppermute | solution.py:17
  35.7 3.3 %collective-permute-start.4 = (bf16[128,512]{1,0:T(8,128)(2,1)S(1)}, bf16[128,512]{1,0:T(8,128)(2,1)S(1)}, u32[]{:S(2)}, u32[]{:S(2)}) collective-permute-start(bf16[128,512]{1,0:T(8,128)(2,1)S(1)} %collective-permute-done.3), channel_id=1, source_target_pairs={{0,1},{1,2},{2,3},{3,4},{4,5},{5,6},{6,7},{7,8},{8,9},{9,10},{10,1... | collective-permute-start | bytes 393224 | tf_op jit(solution)/shard_map/ppermute | solution.py:17
  40.7 1.9 collective-permute-start.12
  42.6 5.1 %collective-permute-start.5 = (bf16[128,512]{1,0:T(8,128)(2,1)S(1)}, bf16[128,512]{1,0:T(8,128)(2,1)S(1)}, u32[]{:S(2)}, u32[]{:S(2)}) collective-permute-start(bf16[128,512]{1,0:T(8,128)(2,1)S(1)} %collective-permute-done.4), channel_id=1, source_target_pairs={{0,1},{1,2},{2,3},{3,4},{4,5},{5,6},{6,7},{7,8},{8,9},{9,10},{10,1... | collective-permute-start | bytes 393224 | tf_op jit(solution)/shard_map/ppermute | solution.py:17
  47.8 3.4 %collective-permute-start.13 = (bf16[128,512]{0,1:T(8,128)(2,1)}, bf16[128,512]{0,1:T(8,128)(2,1)S(1)}, u32[]{:S(2)}, u32[]{:S(2)}) collective-permute-start(bf16[128,512]{0,1:T(8,128)(2,1)} %collective-permute-done.12), channel_id=1, source_target_pairs={{0,1},{1,2},{2,3},{3,4},{4,5},{5,6},{6,7},{7,8},{8,9},{9,10},{10,1... | collective-permute-start | bytes 393224 | tf_op jit(solution)/shard_map/ppermute | solution.py:17
  51.3 5.0 %collective-permute-start.6 = (bf16[128,512]{1,0:T(8,128)(2,1)S(1)}, bf16[128,512]{1,0:T(8,128)(2,1)S(1)}, u32[]{:S(2)}, u32[]{:S(2)}) collective-permute-start(bf16[128,512]{1,0:T(8,128)(2,1)S(1)} %collective-permute-done.5), channel_id=1, source_target_pairs={{0,1},{1,2},{2,3},{3,4},{4,5},{5,6},{6,7},{7,8},{8,9},{9,10},{10,1... | collective-permute-start | bytes 393224 | tf_op jit(solution)/shard_map/ppermute | solution.py:17
  57.0 3.3 %collective-permute-start.14 = (bf16[128,512]{0,1:T(8,128)(2,1)S(1)}, bf16[128,512]{0,1:T(8,128)(2,1)}, u32[]{:S(2)}, u32[]{:S(2)}) collective-permute-start(bf16[128,512]{0,1:T(8,128)(2,1)S(1)} %collective-permute-done.13), channel_id=1, source_target_pairs={{0,1},{1,2},{2,3},{3,4},{4,5},{5,6},{6,7},{7,8},{8,9},{9,10},{10,1... | collective-permute-start | bytes 393224 | tf_op jit(solution)/shard_map/ppermute | solution.py:17
  60.3 5.0 %collective-permute-start.7 = (bf16[128,512]{1,0:T(8,128)(2,1)S(1)}, bf16[128,512]{1,0:T(8,128)(2,1)S(1)}, u32[]{:S(2)}, u32[]{:S(2)}) collective-permute-start(bf16[128,512]{1,0:T(8,128)(2,1)S(1)} %collective-permute-done.6), channel_id=1, source_target_pairs={{0,1},{1,2},{2,3},{3,4},{4,5},{5,6},{6,7},{7,8},{8,9},{9,10},{10,1... | collective-permute-start | bytes 393224 | tf_op jit(solution)/shard_map/ppermute | solution.py:17
  67.2 1.1 copy.88
  68.3 3.0 %collective-permute-start.15 = (bf16[128,512]{0,1:T(8,128)(2,1)}, bf16[128,512]{0,1:T(8,128)(2,1)}, u32[]{:S(2)}, u32[]{:S(2)}) collective-permute-start(bf16[128,512]{0,1:T(8,128)(2,1)} %collective-permute-done.14), channel_id=1, source_target_pairs={{0,1},{1,2},{2,3},{3,4},{4,5},{5,6},{6,7},{7,8},{8,9},{9,10},{10,1... | collective-permute-start | bytes 393224 | tf_op jit(solution)/shard_map/ppermute | solution.py:17
  72.3 4.2 %collective-permute-done.15 = bf16[128,512]{0,1:T(8,128)(2,1)} collective-permute-done((bf16[128,512]{0,1:T(8,128)(2,1)}, bf16[128,512]{0,1:T(8,128)(2,1)}, u32[]{:S(2)}, u32[]{:S(2)}) %collective-permute-start.15) | collective-permute-done | bytes 131104 | tf_op jit(solution)/shard_map/ppermute | solution.py:17
  77.4 0.9 constant_dynamic-update-slice_fusion.16
  78.3 0.9 constant_dynamic-update-slice_fusion.15
  79.3 1.0 constant_dynamic-update-slice_fusion.14
  80.2 0.9 constant_dynamic-update-slice_fusion.13
  81.4 1.0 copy-done.7
  82.4 21.9 %while.11 = (s32[]{:T(128)}, bf16[4,128,5,128]{1,3,2,0:T(8,128)(2,1)S(1)}, bf16[4,1152,128]{1,2,0:T(8,128)(2,1)S(1)}, bf16[4,1152,128]{1,2,0:T(8,128)(2,1)}, bf1...) while((s32[]{:T(128)}, ...), condition=%wide.region_3.4_spmd.clone, body=%wide.region_0.3_spmd.clone.sunk | while | flops 573541248 | bytes 1835245 | solution.py:80
  83.2 2.1 fusion.105
  85.4 2.5 fusion.106
  88.8 2.1 fusion.105
  90.9 2.5 fusion.106
  94.2 2.1 fusion.105
  96.3 2.5 fusion.106
  99.7 2.1 fusion.105
  101.8 2.5 fusion.106
  104.3 17.9 %reshape.217 = bf16[2560,2560]{1,0:T(8,128)(2,1)} reshape(bf16[128,20,2560]{2,1,0:T(8,128)(2,1)} %all-gather.3.cloned.1.call-done) | data formatting | bytes 26214400
  122.2 9.2 %convolution_convert_fusion.2 = bf16[128,2560]{1,0:T(8,128)(2,1)S(1)} fusion(bf16[128,2560]{0,1:T(8,128)(2,1)S(1)} %bitcast.151, bf16[2560,2560]{1,0:T(8,128)(2,1)} %reshape.217), kind=kOutput, calls=%fused_computation.36 | convolution fusion | flops 1678049280 | bytes 14417920 | tf_op jit(solution)/shard_map/dot_general | solution.py:83
  135.0 55.5 %all_to_all.10 = bf16[128,2,2560]{2,1,0:T(2,128)(2,1)S(1)} all-to-all(bf16[128,2,2560]{2,1,0:T(2,128)(2,1)S(1)} %reshape.211), channel_id=1, replica_groups=mesh['seq'=128] {'seq'}, dimensions={0} | all-to-all | bytes 2621440 | tf_op jit(solution)/shard_map/all_to_all | solution.py:114
  190.5 1.0 collective-permute-start.16
  191.4 2.7 %collective-permute-done.16 = bf16[128,2,2560]{2,1,0:T(2,128)(2,1)S(1)} collective-permute-done((bf16[128,2,2560]{2,1,0:T(2,128)(2,1)S(1)}, bf16[128,2,2560]{2,1,0:T(2,128)(2,1)S(1)}, u32[]{:S(2)}, u32[]{:S(2)}) %collective-permute-start.16) | collective-permute-done | bytes 1310752 | tf_op jit(solution)/shard_map/ppermute | solution.py:23
  194.1 2.0 fusion.62
  196.1 3.7 %pad_maximum_fusion = bf16[128,2,2,2560]{3,2,0,1:T(2,128)(2,1)S(1)} fusion(bf16[128,1,2,2560]{3,2,0,1:T(2,128)(2,1)S(1)} %get-tuple-element.122, bf16[128,1,2,2560]{3,2,0,1:T(2,128)(2,1)S(1)} %get-tuple-element.121), kind=kLoop, calls=%fused_computation.37 | loop fusion | flops 1310720 | bytes 5242880 | tf_op jit(solution)/shard_map/stack | solution.py:119
  200.1 7.2 %fusion.55 = f32[2,1,128,4,832]{2,4,0,3,1:T(8,128)S(1)} fusion(bf16[128,4,2560,1]{2,0,3,1:T(8,128)(2,1)S(1)} %bitcast.149, bf16[2560,2,832]{0,2,1:T(8,128)(2,1)} %param.20), kind=kOutput, calls=%fused_computation.44 | convolution fusion | flops 4362076160 | bytes 14548992 | tf_op jit(solution)/shard_map/nlkd,dglf->glnkf/dot_general | solution.py:120
  207.4 3.3 %fusion.51 = bf16[128,1,4,2560]{3,0,2,1:T(8,128)(2,1)S(1)} fusion(bf16[832,2560]{1,0:T(8,128)(2,1)S(1)} %bitcast.159, f32[2,1,128,4,832]{2,4,0,3,1:T(8,128)S(1)} %fusion.55), kind=kOutput, calls=%fused_computation.34 | convolution fusion | flops 2184904704 | bytes 10289152 | tf_op jit(solution)/shard_map/lnkf,lfd->nlkd/dot_general | solution.py:124
  210.9 2.2 fusion.61
  213.8 2.7 %collective-permute-done.17 = bf16[128,2,2560]{2,1,0:T(2,128)(2,1)S(1)} collective-permute-done((bf16[128,2,2560]{2,1,0:T(2,128)(2,1)S(1)}, bf16[128,2,2560]{2,1,0:T(2,128)(2,1)S(1)}, u32[]{:S(2)}, u32[]{:S(2)}) %collective-permute-start.17) | collective-permute-done | bytes 1310752 | tf_op jit(solution)/shard_map/ppermute | solution.py:23
  216.4 7.5 %fusion.54 = bf16[128,2,2560]{2,1,0:T(2,128)(2,1)} fusion(bf16[128,2,2560]{2,1,0:T(2,128)(2,1)S(1)} %collective-permute-done.17, pred[]{:T(512)S(6)} %eq.68, bf16[128,1,2,2560]{3,0,2,1:T(8,128)(2,1)S(1)} %get-tuple-element.120, bf16[128,1,2,2560]{3,0,2,1:T(8,128)(2,1)S(1)} %get-tuple-element.119), kind=kLoop, calls=%fused_computation.39 | loop fusion | flops 3276800 | bytes 5242881 | tf_op jit(solution)/shard_map/convert_element_type | solution.py:133
  224.0 3.9 %all-to-all-start.1 = ((bf16[128,2,2560]{2,1,0:T(2,128)(2,1)}), bf16[128,2,2560]{2,1,0:T(2,128)(2,1)S(1)}, u32[]{:S(2)}, u32[]{:S(2)}) async-start(bf16[128,2,2560]{2,1,0:T(2,128)(2,1)} %fusion.54), calls=%async_computation.1 | async-start | bytes 2621440 | tf_op jit(solution)/shard_map/all_to_all | solution.py:134
  228.2 21.9 %all-to-all-done.1 = bf16[128,2,2560]{2,1,0:T(2,128)(2,1)S(1)} async-done(((bf16[128,2,2560]{2,1,0:T(2,128)(2,1)}), bf16[128,2,2560]{2,1,0:T(2,128)(2,1)S(1)}, u32[]{:S(2)}, u32[]{:S(2)}) %all-to-all-start.1) | async-done | bytes 1310752 | tf_op jit(solution)/shard_map/all_to_all | solution.py:134
  250.6 1.4 fusion.59
  (127 shorter events, 17.9 us)
Async XLA Ops:
  7.2 40.6 %copy-start.19 = (s32[128]{0:T(128)S(1)}, s32[128]{0:T(128)}, u32[]{:S(2)}) copy-start(s32[128]{0:T(128)} %param.24) | copy-start | bytes 1540
  7.2 49.1 %copy-start.15 = (s32[128,2]{0,1:T(2,128)S(1)}, s32[128,2]{0,1:T(2,128)}, u32[]{:S(2)}) copy-start(s32[128,2]{0,1:T(2,128)} %param.22) | copy-start | bytes 3076
  7.2 60.0 %copy-start.2 = (bf16[128,2560]{1,0:T(8,128)(2,1)S(1)}, bf16[128,2560]{1,0:T(8,128)(2,1)}, u32[]{:S(2)}) copy-start(bf16[128,2560]{1,0:T(8,128)(2,1)} %param.15) | copy-start | bytes 1966084
  7.2 97.1 %all-gather.3.cloned.1.call-start = ((), (), s32[]{:S(2)}) async-start(), calls=%async_computation.2 | async-start | bytes 15851520 | tf_op jit(solution)/shard_map/all_gather | solution.py:82
  7.9 8.2 %collective-permute-start = (bf16[128,512]{1,0:T(8,128)(2,1)}, bf16[128,512]{1,0:T(8,128)(2,1)S(1)}, u32[]{:S(2)}, u32[]{:S(2)}) collective-permute-start(bf16[128,512]{1,0:T(8,128)(2,1)} %param.17), channel_id=1, source_target_pairs={{0,1},{1,2},{2,3},{3,4},{4,5},{5,6},{6,7},{7,8},{8,9},{9,10},{10,1... | collective-permute-start | bytes 393224 | tf_op jit(solution)/shard_map/ppermute | solution.py:17
  13.5 7.5 %collective-permute-start.8 = (bf16[128,512]{0,1:T(8,128)(2,1)S(1)}, bf16[128,512]{0,1:T(8,128)(2,1)S(1)}, u32[]{:S(2)}, u32[]{:S(2)}) collective-permute-start(bf16[128,512]{0,1:T(8,128)(2,1)S(1)} %copy.86), channel_id=1, source_target_pairs={{0,1},{1,2},{2,3},{3,4},{4,5},{5,6},{6,7},{7,8},{8,9},{9,10},{10,1... | collective-permute-start | bytes 393224 | tf_op jit(solution)/shard_map/ppermute | solution.py:17
  16.1 6.7 %collective-permute-start.1 = (bf16[128,512]{1,0:T(8,128)(2,1)S(1)}, bf16[128,512]{1,0:T(8,128)(2,1)S(1)}, u32[]{:S(2)}, u32[]{:S(2)}) collective-permute-start(bf16[128,512]{1,0:T(8,128)(2,1)S(1)} %collective-permute-done), channel_id=1, source_target_pairs={{0,1},{1,2},{2,3},{3,4},{4,5},{5,6},{6,7},{7,8},{8,9},{9,10},{10,1... | collective-permute-start | bytes 393224 | tf_op jit(solution)/shard_map/ppermute | solution.py:17
  20.9 5.4 %collective-permute-start.9 = (bf16[128,512]{0,1:T(8,128)(2,1)S(1)}, bf16[128,512]{0,1:T(8,128)(2,1)S(1)}, u32[]{:S(2)}, u32[]{:S(2)}) collective-permute-start(bf16[128,512]{0,1:T(8,128)(2,1)S(1)} %collective-permute-done.8), channel_id=1, source_target_pairs={{0,1},{1,2},{2,3},{3,4},{4,5},{5,6},{6,7},{7,8},{8,9},{9,10},{10,1... | collective-permute-start | bytes 393224 | tf_op jit(solution)/shard_map/ppermute | solution.py:17
  22.9 6.3 %collective-permute-start.2 = (bf16[128,512]{1,0:T(8,128)(2,1)S(1)}, bf16[128,512]{1,0:T(8,128)(2,1)S(1)}, u32[]{:S(2)}, u32[]{:S(2)}) collective-permute-start(bf16[128,512]{1,0:T(8,128)(2,1)S(1)} %collective-permute-done.1), channel_id=1, source_target_pairs={{0,1},{1,2},{2,3},{3,4},{4,5},{5,6},{6,7},{7,8},{8,9},{9,10},{10,1... | collective-permute-start | bytes 393224 | tf_op jit(solution)/shard_map/ppermute | solution.py:17
  26.3 6.1 %collective-permute-start.10 = (bf16[128,512]{0,1:T(8,128)(2,1)S(1)}, bf16[128,512]{0,1:T(8,128)(2,1)S(1)}, u32[]{:S(2)}, u32[]{:S(2)}) collective-permute-start(bf16[128,512]{0,1:T(8,128)(2,1)S(1)} %collective-permute-done.9), channel_id=1, source_target_pairs={{0,1},{1,2},{2,3},{3,4},{4,5},{5,6},{6,7},{7,8},{8,9},{9,10},{10,1... | collective-permute-start | bytes 393224 | tf_op jit(solution)/shard_map/ppermute | solution.py:17
  29.2 6.6 %collective-permute-start.3 = (bf16[128,512]{1,0:T(8,128)(2,1)S(1)}, bf16[128,512]{1,0:T(8,128)(2,1)S(1)}, u32[]{:S(2)}, u32[]{:S(2)}) collective-permute-start(bf16[128,512]{1,0:T(8,128)(2,1)S(1)} %collective-permute-done.2), channel_id=1, source_target_pairs={{0,1},{1,2},{2,3},{3,4},{4,5},{5,6},{6,7},{7,8},{8,9},{9,10},{10,1... | collective-permute-start | bytes 393224 | tf_op jit(solution)/shard_map/ppermute | solution.py:17
  32.4 8.2 %collective-permute-start.11 = (bf16[128,512]{0,1:T(8,128)(2,1)S(1)}, bf16[128,512]{0,1:T(8,128)(2,1)S(1)}, u32[]{:S(2)}, u32[]{:S(2)}) collective-permute-start(bf16[128,512]{0,1:T(8,128)(2,1)S(1)} %collective-permute-done.10), channel_id=1, source_target_pairs={{0,1},{1,2},{2,3},{3,4},{4,5},{5,6},{6,7},{7,8},{8,9},{9,10},{10,1... | collective-permute-start | bytes 393224 | tf_op jit(solution)/shard_map/ppermute | solution.py:17
  35.7 6.9 %collective-permute-start.4 = (bf16[128,512]{1,0:T(8,128)(2,1)S(1)}, bf16[128,512]{1,0:T(8,128)(2,1)S(1)}, u32[]{:S(2)}, u32[]{:S(2)}) collective-permute-start(bf16[128,512]{1,0:T(8,128)(2,1)S(1)} %collective-permute-done.3), channel_id=1, source_target_pairs={{0,1},{1,2},{2,3},{3,4},{4,5},{5,6},{6,7},{7,8},{8,9},{9,10},{10,1... | collective-permute-start | bytes 393224 | tf_op jit(solution)/shard_map/ppermute | solution.py:17
  40.5 26.7 %copy-start.10 = (s32[256]{0:T(256)}, s32[256]{0:T(256)S(1)}, u32[]{:S(2)}) copy-start(s32[256]{0:T(256)S(1)} %get-tuple-element.95) | copy-start | bytes 3076
  40.7 26.5 %copy-start.12 = (s32[128,2]{0,1:T(2,128)}, s32[128,2]{0,1:T(2,128)S(1)}, u32[]{:S(2)}) copy-start(s32[128,2]{0,1:T(2,128)S(1)} %copy.96) | copy-start | bytes 3076
  40.7 30.7 %copy-start.5 = (bf16[128,512]{0,1:T(8,128)(2,1)}, bf16[128,512]{0,1:T(8,128)(2,1)S(1)}, u32[]{:S(2)}) copy-start(bf16[128,512]{0,1:T(8,128)(2,1)S(1)} %collective-permute-done.11) | copy-start | bytes 393220
  40.7 7.1 %collective-permute-start.12 = (bf16[128,512]{0,1:T(8,128)(2,1)S(1)}, bf16[128,512]{0,1:T(8,128)(2,1)}, u32[]{:S(2)}, u32[]{:S(2)}) collective-permute-start(bf16[128,512]{0,1:T(8,128)(2,1)S(1)} %collective-permute-done.11), channel_id=1, source_target_pairs={{0,1},{1,2},{2,3},{3,4},{4,5},{5,6},{6,7},{7,8},{8,9},{9,10},{10,1... | collective-permute-start | bytes 393224 | tf_op jit(solution)/shard_map/ppermute | solution.py:17
  42.6 8.6 %collective-permute-start.5 = (bf16[128,512]{1,0:T(8,128)(2,1)S(1)}, bf16[128,512]{1,0:T(8,128)(2,1)S(1)}, u32[]{:S(2)}, u32[]{:S(2)}) collective-permute-start(bf16[128,512]{1,0:T(8,128)(2,1)S(1)} %collective-permute-done.4), channel_id=1, source_target_pairs={{0,1},{1,2},{2,3},{3,4},{4,5},{5,6},{6,7},{7,8},{8,9},{9,10},{10,1... | collective-permute-start | bytes 393224 | tf_op jit(solution)/shard_map/ppermute | solution.py:17
  47.8 9.1 %collective-permute-start.13 = (bf16[128,512]{0,1:T(8,128)(2,1)}, bf16[128,512]{0,1:T(8,128)(2,1)S(1)}, u32[]{:S(2)}, u32[]{:S(2)}) collective-permute-start(bf16[128,512]{0,1:T(8,128)(2,1)} %collective-permute-done.12), channel_id=1, source_target_pairs={{0,1},{1,2},{2,3},{3,4},{4,5},{5,6},{6,7},{7,8},{8,9},{9,10},{10,1... | collective-permute-start | bytes 393224 | tf_op jit(solution)/shard_map/ppermute | solution.py:17
  51.3 9.0 %collective-permute-start.6 = (bf16[128,512]{1,0:T(8,128)(2,1)S(1)}, bf16[128,512]{1,0:T(8,128)(2,1)S(1)}, u32[]{:S(2)}, u32[]{:S(2)}) collective-permute-start(bf16[128,512]{1,0:T(8,128)(2,1)S(1)} %collective-permute-done.5), channel_id=1, source_target_pairs={{0,1},{1,2},{2,3},{3,4},{4,5},{5,6},{6,7},{7,8},{8,9},{9,10},{10,1... | collective-permute-start | bytes 393224 | tf_op jit(solution)/shard_map/ppermute | solution.py:17
  56.9 14.4 %copy-start.6 = (bf16[128,512]{0,1:T(8,128)(2,1)}, bf16[128,512]{0,1:T(8,128)(2,1)S(1)}, u32[]{:S(2)}) copy-start(bf16[128,512]{0,1:T(8,128)(2,1)S(1)} %collective-permute-done.13) | copy-start | bytes 393220
  57.0 11.3 %collective-permute-start.14 = (bf16[128,512]{0,1:T(8,128)(2,1)S(1)}, bf16[128,512]{0,1:T(8,128)(2,1)}, u32[]{:S(2)}, u32[]{:S(2)}) collective-permute-start(bf16[128,512]{0,1:T(8,128)(2,1)S(1)} %collective-permute-done.13), channel_id=1, source_target_pairs={{0,1},{1,2},{2,3},{3,4},{4,5},{5,6},{6,7},{7,8},{8,9},{9,10},{10,1... | collective-permute-start | bytes 393224 | tf_op jit(solution)/shard_map/ppermute | solution.py:17
  60.3 11.0 %collective-permute-start.7 = (bf16[128,512]{1,0:T(8,128)(2,1)S(1)}, bf16[128,512]{1,0:T(8,128)(2,1)S(1)}, u32[]{:S(2)}, u32[]{:S(2)}) collective-permute-start(bf16[128,512]{1,0:T(8,128)(2,1)S(1)} %collective-permute-done.6), channel_id=1, source_target_pairs={{0,1},{1,2},{2,3},{3,4},{4,5},{5,6},{6,7},{7,8},{8,9},{9,10},{10,1... | collective-permute-start | bytes 393224 | tf_op jit(solution)/shard_map/ppermute | solution.py:17
  68.3 3.2 %copy-start.4 = (bf16[128,512]{1,0:T(8,128)(2,1)S(1)}, bf16[128,512]{1,0:T(8,128)(2,1)}, u32[]{:S(2)}) copy-start(bf16[128,512]{1,0:T(8,128)(2,1)} %param.17) | copy-start | bytes 393220
  68.3 8.2 %collective-permute-start.15 = (bf16[128,512]{0,1:T(8,128)(2,1)}, bf16[128,512]{0,1:T(8,128)(2,1)}, u32[]{:S(2)}, u32[]{:S(2)}) collective-permute-start(bf16[128,512]{0,1:T(8,128)(2,1)} %collective-permute-done.14), channel_id=1, source_target_pairs={{0,1},{1,2},{2,3},{3,4},{4,5},{5,6},{6,7},{7,8},{8,9},{9,10},{10,1... | collective-permute-start | bytes 393224 | tf_op jit(solution)/shard_map/ppermute | solution.py:17
  72.2 10.1 %copy-start.3 = (bf16[128,2560]{0,1:T(8,128)(2,1)S(1)}, bf16[128,2560]{0,1:T(8,128)(2,1)}, u32[]{:S(2)}) copy-start(bf16[128,2560]{0,1:T(8,128)(2,1)} %copy.88) | copy-start | bytes 1966084
  72.3 10.1 %copy-start.8 = (s32[128]{0:T(128)S(1)}, s32[128]{0:T(128)}, u32[]{:S(2)}) copy-start(s32[128]{0:T(128)} %get-tuple-element.188) | copy-start | bytes 1540
  81.3 1.0 copy-start.7
  122.2 9.2 %copy-start.1 = (bf16[128,2560]{1,0:T(8,128)(2,1)S(1)}, bf16[128,2560]{1,0:T(8,128)(2,1)}, u32[]{:S(2)}) copy-start(bf16[128,2560]{1,0:T(8,128)(2,1)} %param.14) | copy-start | bytes 1966084
  131.4 1.0 copy-start
  131.4 0.7 copy-start.9
  133.1 0.7 copy-start.14
  133.1 0.7 copy-start.16
  190.5 3.6 %collective-permute-start.16 = (bf16[128,2,2560]{2,1,0:T(2,128)(2,1)S(1)}, bf16[128,2,2560]{2,1,0:T(2,128)(2,1)S(1)}, u32[]{:S(2)}, u32[]{:S(2)}) collective-permute-start(bf16[128,2,2560]{2,1,0:T(2,128)(2,1)S(1)} %all_to_all.10), channel_id=1, source_target_pairs={{0,1},{1,0},{2,3},{3,2},{4,5},{5,4},{6,7},{7,6},{8,9},{9,8},{10,11... | collective-permute-start | bytes 3932168 | tf_op jit(solution)/shard_map/ppermute | solution.py:23
  199.8 7.5 %slice-start = ((s8[4259840]{0:T(1024)(128)(4,1)}), s8[4194304]{0:T(1024)(128)(4,1)S(1)}, s32[]{:S(2)}) async-start(s8[4259840]{0:T(1024)(128)(4,1)} %bitcast.158), calls=%async_computation.3 | async-start | bytes 8388608
  200.1 7.2 %slice-start.1 = ((s8[4259840]{0:T(1024)(128)(4,1)}), s8[65536]{0:T(1024)(128)(4,1)S(1)}, s32[]{:S(2)}) async-start(s8[4259840]{0:T(1024)(128)(4,1)} %bitcast.158), calls=%async_computation.4 | async-start | bytes 131072
  213.1 3.3 %collective-permute-start.17 = (bf16[128,2,2560]{2,1,0:T(2,128)(2,1)S(1)}, bf16[128,2,2560]{2,1,0:T(2,128)(2,1)S(1)}, u32[]{:S(2)}, u32[]{:S(2)}) collective-permute-start(bf16[128,2,2560]{2,1,0:T(2,128)(2,1)S(1)} %fusion.61), channel_id=1, source_target_pairs={{0,1},{1,0},{2,3},{3,2},{4,5},{5,4},{6,7},{7,6},{8,9},{9,8},{10,11... | collective-permute-start | bytes 3932168 | tf_op jit(solution)/shard_map/ppermute | solution.py:23
  223.9 3.9 %copy-start.11 = (s32[256]{0:T(256)S(1)}, s32[256]{0:T(256)}, u32[]{:S(2)}) copy-start(s32[256]{0:T(256)} %copy-done.10) | copy-start | bytes 3076
  224.0 4.2 %copy-start.13 = (s32[128,2]{0,1:T(2,128)S(1)}, s32[128,2]{0,1:T(2,128)}, u32[]{:S(2)}) copy-start(s32[128,2]{0,1:T(2,128)} %copy-done.12) | copy-start | bytes 3076
  224.0 4.2 %copy-start.17 = (s32[128,2]{0,1:T(2,128)S(1)}, s32[128,2]{0,1:T(2,128)}, u32[]{:S(2)}) copy-start(s32[128,2]{0,1:T(2,128)} %param.23) | copy-start | bytes 3076
  224.0 26.1 %all-to-all-start.1 = ((bf16[128,2,2560]{2,1,0:T(2,128)(2,1)}), bf16[128,2,2560]{2,1,0:T(2,128)(2,1)S(1)}, u32[]{:S(2)}, u32[]{:S(2)}) async-start(bf16[128,2,2560]{2,1,0:T(2,128)(2,1)} %fusion.54), calls=%async_computation.1 | async-start | bytes 2621440 | tf_op jit(solution)/shard_map/all_to_all | solution.py:134
  228.1 22.5 %copy-start.18 = (s32[128,2]{0,1:T(2,128)S(1)}, s32[128,2]{0,1:T(2,128)}, u32[]{:S(2)}) copy-start(s32[128,2]{0,1:T(2,128)} %get-tuple-element.115) | copy-start | bytes 3076
Sparse Core Ops, SparseCore 0:
  11.0 86.0 all-gather.2
where the time goes:
time: 260 us; the launch traced here: 259 us
  starting transfers between devices  60.1 us (23%)
  blocking collectives  55.5 us (21%)
  matrix products  40.1 us (15%)
  local copies, waits for them, and re-layouts  33.2 us (13%)
  waiting for transfers between devices  32.2 us (12%)
  other arithmetic  22.9 us (9%)
  between operations  14.8 us (6%)
    all_to_all x1, blocking collectives, body(): lax.all_to_all(outgoing, 'seq', split_axis=0, concat_axis=0, tiled=True)  55.5 us
    ppermute x16, starting transfers between devices, shifted(): lax.ppermute(value, axis, [(source, source + steps) for source in range(i...  54.5 us
    unnamed x65, local copies, waits for them, and re-layouts  27.3 us
    all_to_all x1, waiting for transfers between devices, body(): lax.all_to_all(summed, 'seq', split_axis=0, concat_axis=0, tiled=True)  21.9 us
    dot_general x4, matrix products, one_head(): jnp.einsum('gqk,kd->qgd', probs_bf, v_one, preferred_element_type=jnp.flo...  9.96 us
    dot_general x1, matrix products, body(): jnp.dot(context, whole_proj, preferred_element_type=jnp.float32)  9.15 us
    sub x4, matrix products, one_head(): weights_raw = jnp.exp(scores - row_max)  8.38 us
    convert_element_type x1, other arithmetic, body(): (keep_own.astype(jnp.float32) + taken.astype(jnp.float32)).astype(jnp.bfl...  7.52 us
  transfers between devices with their start and end apart: 20, of which 4 were waited for; matrix products, arithmetic and copies ran while one was open for 14% of the time, Pallas kernels for 0%

commit v1 on v0

v1 whole, which is shorter than its diff:
```python
import functools

import jax
import jax.numpy as jnp
from jax import lax
from jax.experimental import pallas as pl
from jax.experimental.pallas import tpu as pltpu
from jax.sharding import PartitionSpec as P

HEADS = 20
KV_HEADS = 4
HEAD = 128
GROUP = HEADS // KV_HEADS
WINDOW = 1024
EXPERTS = 64
CAP = 2
D = 2560
TOK = 128
NDEV = 128
MESH = pl.DeviceIdType.MESH
DMA = pltpu.SemaphoreType.DMA
DELTAS = (1, 3, 2)
PARTS = (((2, 1, 0), 0, 7), ((1, 0, 2), 7, 5), ((0, 2, 1), 12, 8))
KT = D // 128


def coords(me):
    return [me // 32, (me // 8) % 4, (me // 2) % 4, me % 2]


def dev(cs):
    return ((cs[0] * 4 + cs[1]) * 4 + cs[2]) * 2 + cs[3]


def shift(cs, dim, d):
    cs = list(cs)
    cs[dim] = lax.rem(cs[dim] + d, 4)
    return cs


def wslice(cs, alld, fixed, t0, tn):
    idx = [slice(None) if d in alld else cs[d] for d in range(3)]
    for d, v in fixed.items():
        idx[d] = v
    return tuple(idx) + (pl.ds(t0, tn),)


def attend_kernel(
    wa, wb, q, k, v, res, gain, att_out, norm_out,
    G, B1, BX, Kb, Vb, bias, ctx, attp, attt,
    s1, r1, s2, r2, s3, r3, s4, r4, sb1, rb1, sb2, rb2, sb3, rb3, sb4, rb4,
    kvs, kvr, cxs, cxr, ats, atr, lsem,
):
    me = lax.axis_index("seq")
    cs = coords(me)
    y, z, x, core = cs
    bar = pltpu.get_barrier_semaphore()
    sib = dev([y, z, x, 1 - core])
    peers = [dev(shift(cs, dim, d)) for dim in range(3) for d in DELTAS]
    peers += [sib, lax.rem(me + 8, NDEV), lax.rem(me + NDEV - 8, NDEV)]
    for p in peers:
        pl.semaphore_signal(bar, inc=1, device_id=(p,), device_id_type=MESH)
    own = [
        pltpu.make_async_copy(wa, G.at[y, z, x], lsem.at[0]),
        pltpu.make_async_copy(wb, B1.at[x], lsem.at[1]),
        pltpu.make_async_copy(k, Kb.at[8], lsem.at[2]),
        pltpu.make_async_copy(v, Vb.at[8], lsem.at[3]),
    ]
    for c in own:
        c.start()
    row = lax.broadcasted_iota(jnp.int32, (TOK, TOK), 0)
    col = lax.broadcasted_iota(jnp.int32, (TOK, TOK), 1)
    for j in range(9):
        ok = me - 8 + j >= 0
        if j == 0:
            m = (col > row) & ok
        elif j == 8:
            m = col <= row
        else:
            m = (col >= 0) & ok
        bias[:, j * TOK:(j + 1) * TOK] = jnp.where(m, 0.0, -jnp.inf)
    for c in own:
        c.wait()
    pl.semaphore_wait(bar, len(peers))
    sends = []

    def rc(src, dst, ss, rs, dv):
        c = pltpu.make_async_remote_copy(
            src_ref=src, dst_ref=dst, send_sem=ss, recv_sem=rs, device_id=(dv,), device_id_type=MESH
        )
        c.start()
        sends.append(c)
        return c

    nxt = lax.rem(me + 8, NDEV)
    kv4 = [rc(b_.at[8], b_.at[0], kvs.at[n, 3], kvr.at[n, 3], nxt) for n, b_ in enumerate((Kb, Vb))]
    kvx = []
    for dlt in (1, 2, 3):
        tgt = dev(shift(cs, 2, dlt))
        pair = []
        for n, b_ in enumerate((Kb, Vb)):
            pair.append(
                tuple(
                    pltpu.make_async_remote_copy(
                        src_ref=b_.at[s], dst_ref=b_.at[8 - 2 * dlt], send_sem=kvs.at[n, dlt - 1],
                        recv_sem=kvr.at[n, dlt - 1], device_id=(tgt,), device_id_type=MESH,
                    )
                    for s in (8, 0)
                )
            )
        kvx.append(pair)
        sends += [p_[0] for p_ in pair]

        @pl.when(x + dlt < 4)
        def _():
            for p_ in pair:
                p_[0].start()

    p1 = []
    for pi, ((a, bb, c), t0, tn) in enumerate(PARTS):
        sl = wslice(cs, (), {}, t0, tn)
        p1.append(
            [rc(G.at[sl], G.at[sl], s1.at[pi, i], r1.at[pi, i], dev(shift(cs, a, d))) for i, d in enumerate(DELTAS)]
        )
    pb1 = [rc(B1.at[x], B1.at[x], sb1.at[i], rb1.at[i], dev(shift(cs, 2, d))) for i, d in enumerate(DELTAS)]

    p3 = [[None] * 4 for _ in PARTS]
    pb3 = [None] * 4

    def chunk_send(pi, i, bi):
        (a, bb, c), t0, tn = PARTS[pi]
        sl = wslice(cs, (a,), {bb: bi}, t0, tn)
        p3[pi][i] = [
            rc(G.at[sl], G.at[sl], s3.at[pi, i, n], r3.at[pi, i, n], dev(shift(cs, c, d)))
            for n, d in enumerate(DELTAS[:2])
        ]
        if pi == 0:
            pb3[i] = [
                rc(BX.at[y, bi], BX.at[y, bi], sb3.at[i, n], rb3.at[i, n], dev(shift(cs, 0, d)))
                for n, d in enumerate(DELTAS[:2])
            ]

    p2 = []
    pb2 = []
    for pi, ((a, bb, c), t0, tn) in enumerate(PARTS):
        for n in range(3):
            p1[pi][n].wait_recv()
        if pi == 0:
            for n in range(3):
                pb1[n].wait_recv()
            src = [[B1[xx, i].astype(jnp.float32) for i in range(5)] for xx in range(4)]
            for kq in range(4):
                for i in range(5):
                    BX[y, z, kq * 5 + i] = jnp.concatenate(
                        [src[xx][i][kq * 4:kq * 4 + 4] for xx in range(4)], 0
                    ).astype(jnp.bfloat16)
        sl = wslice(cs, (a,), {}, t0, tn)
        p2.append(
            [rc(G.at[sl], G.at[sl], s2.at[pi, i], r2.at[pi, i], dev(shift(cs, bb, d))) for i, d in enumerate(DELTAS)]
        )
        if pi == 0:
            pb2 = [
                rc(BX.at[y, z], BX.at[y, z], sb2.at[i], rb2.at[i], dev(shift(cs, 1, d)))
                for i, d in enumerate(DELTAS)
            ]
        chunk_send(pi, 0, cs[bb])

    for c in kv4:
        c.wait_recv()
    for dlt in (1, 2, 3):

        @pl.when(x + dlt >= 4)
        def _():
            for p_ in kvx[dlt - 1]:
                p_[1].start()

    for i, d in enumerate(DELTAS):
        for pi, ((a, bb, c), t0, tn) in enumerate(PARTS):
            p2[pi][i].wait_recv()
            if pi == 0:
                pb2[i].wait_recv()
            chunk_send(pi, i + 1, lax.rem(cs[bb] + 4 - d, 4))

    rl = []

    def relay(i):
        for pi, ((a, bb, c), t0, tn) in enumerate(PARTS):
            bi = cs[bb] if i == 0 else lax.rem(cs[bb] + 4 - DELTAS[i - 1], 4)
            h = tn // 2
            for n, (dfrom, dto, lo, cnt) in enumerate(((3, 1, 0, h), (1, 3, h, tn - h))):
                p3[pi][i][n].wait_recv()
                s_ = wslice(cs, (a,), {bb: bi, c: lax.rem(cs[c] + dfrom, 4)}, t0 + lo, cnt)
                rl.append(rc(G.at[s_], G.at[s_], s4.at[pi, i, n], r4.at[pi, i, n], dev(shift(cs, c, dto))))
                if pi == 0:
                    pb3[i][n].wait_recv()
                    b_ = BX.at[lax.rem(y + dfrom, 4), bi, pl.ds(10 * n, 10)]
                    rl.append(rc(b_, b_, sb4.at[i, n], rb4.at[i, n], dev(shift(cs, 0, dto))))

    relay(0)
    kvd = []
    for p_ in kvx:
        for n in range(2):
            p_[n][0].wait_recv()
    for i in range(4):
        src = 8 - 2 * i - 2 * core
        for n, b_ in enumerate((Kb, Vb)):
            kvd.append(rc(b_.at[src], b_.at[7 - 2 * i], kvs.at[n, 4 + i], kvr.at[n, 4 + i], sib))
    relay(1)
    for c in kvd:
        c.wait_recv()

    scale = HEAD ** (-0.5)
    cxc = []
    for h in range(KV_HEADS):
        hs = slice(h * HEAD, (h + 1) * HEAD)
        kh = Kb[:, :, hs].reshape(9 * TOK, HEAD)
        vh = Vb[:, :, hs].reshape(9 * TOK, HEAD)
        for g in range(GROUP):
            qs = slice((h * GROUP + g) * HEAD, (h * GROUP + g + 1) * HEAD)
            s = lax.dot_general(
                q[:, qs], kh, (((1,), (1,)), ((), ())), preferred_element_type=jnp.float32
            ) * scale + bias[...]
            mx = jnp.max(s, -1, keepdims=True)
            e = jnp.exp(s - mx)
            tot = jnp.sum(e, -1, keepdims=True)
            o = jnp.dot(e.astype(jnp.bfloat16), vh, preferred_element_type=jnp.float32)
            ctx[core, h, :, g * HEAD:(g + 1) * HEAD] = (o / tot).astype(jnp.bfloat16)
        cxc.append(rc(ctx.at[core, h], ctx.at[core, h], cxs.at[h], cxr.at[h], sib))
        if h < 2:
            relay(h + 2)
    for c in cxc:
        c.wait_recv()
    for c in rl:
        c.wait_recv()

    def project(tile_pair):
        acc = None
        for kp in range(KT // 2):
            lhs = tile_pair(2 * kp)
            h, off = (2 * kp) // GROUP, (2 * kp) % GROUP
            cols = []
            for t in (2 * kp, 2 * kp + 1):
                hh, oo = t // GROUP, t % GROUP
                cols.append(ctx[:, hh, :, oo * HEAD:(oo + 1) * HEAD].reshape(2 * TOK, HEAD))
            rhs = jnp.concatenate(cols, 1)
            part = lax.dot_general(lhs, rhs, (((1,), (1,)), ((), ())), preferred_element_type=jnp.float32)
            acc = part if acc is None else acc + part
        return acc.astype(jnp.bfloat16)

    def put(first, rows, val):
        attp[core, 0, pl.ds(first, rows)] = val[:, :TOK]
        attp[core, 1, pl.ds(first, rows)] = val[:, TOK:]

    def a_rows(yy, carry):
        def pair(t):
            return jnp.concatenate(
                [G[yy, :, :, t + i].reshape(256, 128) for i in range(2)], 1
            )
        put(yy * 256, 256, project(pair))
        return carry

    lax.fori_loop(0, 4, a_rows, 0)
    put(1024, 256, project(
        lambda t: jnp.concatenate([BX[:, :, t + i].reshape(256, 128) for i in range(2)], 1)
    ))
    xc = rc(attp.at[core, 1 - core], attp.at[core, 1 - core], ats, atr, sib)
    xc.wait_recv()
    mine = [attp.at[0, core], attp.at[1, core]]
    for chip in range(64):
        for c in range(2):
            d0 = 20 * (chip * 2 + c)
            attt[d0:d0 + 16] = mine[c][chip * 16:chip * 16 + 16].astype(jnp.float32)
    for yz in range(16):
        for c in range(2):
            blk = mine[c][1024 + yz * 16:1024 + yz * 16 + 16].astype(jnp.float32)
            for xx in range(4):
                d0 = 20 * ((yz * 4 + xx) * 2 + c) + 16
                attt[d0:d0 + 4] = blk[xx * 4:xx * 4 + 4]
    ssq = jnp.zeros((TOK, 1), jnp.float32)
    for t in range(KT):
        ls = slice(t * 128, (t + 1) * 128)
        a_ = jnp.transpose(attt[ls])
        att_out[:, ls] = a_.astype(jnp.bfloat16)
        hd = res[:, ls].astype(jnp.float32) + a_
        ssq = ssq + jnp.sum(hd * hd, -1, keepdims=True)
    inv = lax.rsqrt(ssq / D + 1e-05)
    for t in range(KT):
        ls = slice(t * 128, (t + 1) * 128)
        hd = res[:, ls].astype(jnp.float32) + att_out[:, ls].astype(jnp.float32)
        norm_out[:, ls] = (hd * inv * gain[:, ls]).astype(jnp.bfloat16)
    for c in sends:
        c.wait_send()


def attend(residual, queries, keys, values, out_proj, norm_gain):
    wt = out_proj.T
    wa = wt[:16].reshape(16, KT, 128).transpose(1, 0, 2)
    wb = wt[16:].reshape(4, 4, 5, 128).transpose(2, 1, 0, 3).reshape(5, 16, 128)
    any_ = pl.BlockSpec(memory_space=pl.ANY)
    vm = pl.BlockSpec(memory_space=pltpu.VMEM)
    bf = jnp.bfloat16
    return pl.pallas_call(
        attend_kernel,
        out_shape=(jax.ShapeDtypeStruct((TOK, D), bf), jax.ShapeDtypeStruct((TOK, D), bf)),
        in_specs=[any_, any_, vm, any_, any_, vm, vm],
        out_specs=(vm, vm),
        scratch_shapes=[
            pltpu.VMEM((4, 4, 4, KT, 16, 128), bf),
            pltpu.VMEM((4, 5, 16, 128), bf),
            pltpu.VMEM((4, 4, KT, 16, 128), bf),
            pltpu.VMEM((9, TOK, KV_HEADS * HEAD), bf),
            pltpu.VMEM((9, TOK, KV_HEADS * HEAD), bf),
            pltpu.VMEM((TOK, 9 * TOK), jnp.float32),
            pltpu.VMEM((2, KV_HEADS, TOK, GROUP * HEAD), bf),
            pltpu.VMEM((2, 2, 1280, TOK), bf),
            pltpu.VMEM((D, TOK), jnp.float32),
            DMA((3, 3)), DMA((3, 3)), DMA((3, 3)), DMA((3, 3)),
            DMA((3, 4, 2)), DMA((3, 4, 2)), DMA((3, 4, 2)), DMA((3, 4, 2)),
            DMA((3,)), DMA((3,)), DMA((3,)), DMA((3,)),
            DMA((4, 2)), DMA((4, 2)), DMA((4, 2)), DMA((4, 2)),
            DMA((2, 8)), DMA((2, 8)), DMA((4,)), DMA((4,)), DMA, DMA, DMA((4,)),
        ],
        compiler_params=pltpu.CompilerParams(
            has_side_effects=True, collective_id=0, vmem_limit_bytes=48 * 2**20
        ),
    )(wa, wb, queries, keys, values, residual, norm_gain.reshape(1, D))


def exchange_kernel(x, o, ssem, rsem, lsem):
    me = lax.axis_index("seq")
    bar = pltpu.get_barrier_semaphore()

    def signal(s, c):
        pl.semaphore_signal(bar, inc=1, device_id=(lax.rem(me + s, NDEV),), device_id_type=MESH)
        return c

    lax.fori_loop(1, NDEV, signal, 0)
    pl.semaphore_wait(bar, NDEV - 1)
    own = pltpu.make_async_copy(x.at[me], o.at[me], lsem)
    own.start()
    cs = coords(me)

    def send(i, c):
        s = (i * 37) % NDEV
        t = dev([(cs[0] + s // 32) % 4, (cs[1] + (s // 8) % 4) % 4, (cs[2] + (s // 2) % 4) % 4, (cs[3] + s % 2) % 2])
        pltpu.make_async_remote_copy(
            src_ref=x.at[t], dst_ref=o.at[me], send_sem=ssem, recv_sem=rsem, device_id=(t,), device_id_type=MESH
        ).start()
        return c

    lax.fori_loop(1, NDEV, send, 0)
    own.wait()
    whole = pl.ds(0, NDEV - 1)
    done = pltpu.make_async_remote_copy(
        src_ref=x.at[whole], dst_ref=o.at[whole], send_sem=ssem, recv_sem=rsem,
        device_id=(lax.rem(me + 1, NDEV),), device_id_type=MESH,
    )
    done.wait_send()
    done.wait_recv()


def exchange(rows, cid):
    return pl.pallas_call(
        exchange_kernel,
        out_shape=jax.ShapeDtypeStruct(rows.shape, rows.dtype),
        in_specs=[pl.BlockSpec(memory_space=pl.ANY)],
        out_specs=pl.BlockSpec(memory_space=pl.ANY),
        scratch_shapes=[DMA, DMA, DMA],
        compiler_params=pltpu.CompilerParams(has_side_effects=True, collective_id=cid),
    )(rows)


def swapped(value):
    return lax.ppermute(value, "seq", [(s, s ^ 1) for s in range(NDEV)])


def body(
    residual, queries, keys, values, out_proj, norm_gain, expert_in, expert_down,
    routes, gate_ints, modality, capacity,
):
    device_pos = lax.axis_index("seq")
    attended, normed = attend(residual, queries, keys, values, out_proj, norm_gain)
    slot_count = 2 * CAP
    chosen = routes.reshape(-1)
    modal_flag = jnp.repeat(modality, 2)
    slot_key = chosen * 2 + modal_flag
    onehot = (slot_key[:, None] == jnp.arange(2 * EXPERTS, dtype=jnp.int32)[None, :]).astype(jnp.int32)
    rank_in = jnp.sum((jnp.cumsum(onehot, 0) - onehot) * onehot, 1)
    limit_of = jnp.sum(onehot * capacity.reshape(1, -1), 1)
    kept_mask = rank_in < limit_of
    column = chosen * slot_count + modal_flag * CAP + rank_in
    select = (
        (column[:, None] == jnp.arange(EXPERTS * slot_count, dtype=jnp.int32)[None, :]) & kept_mask[:, None]
    ).astype(jnp.bfloat16)
    doubled = jnp.repeat(normed, 2, axis=0)
    slot_table = lax.dot_general(
        select, doubled, (((0,), (0,)), ((), ())), preferred_element_type=jnp.float32
    ).astype(jnp.bfloat16)
    hidden_each = expert_in.shape[2]
    own_rows = exchange(slot_table.reshape(NDEV, CAP, D), 1)
    partner = swapped(own_rows)
    is_lower = device_pos % 2 == 0
    first_half = jnp.where(is_lower, own_rows, partner)
    second_half = jnp.where(is_lower, partner, own_rows)
    rows_in = jnp.stack([first_half, second_half], 1).reshape(NDEV, slot_count, D)
    gate_up = jnp.einsum("nkd,dgf->gnkf", rows_in, expert_in, preferred_element_type=jnp.float32)
    active = (jax.nn.silu(gate_up[0]) * gate_up[1]).astype(jnp.bfloat16)
    partial_value = jnp.einsum("nkf,fd->nkd", active, expert_down, preferred_element_type=jnp.float32)
    partial_value = lax.optimization_barrier(partial_value.astype(jnp.bfloat16)).reshape(NDEV, 2, CAP, D)
    keep_own = jnp.where(is_lower, partial_value[:, 0], partial_value[:, 1])
    give_back = jnp.where(is_lower, partial_value[:, 1], partial_value[:, 0])
    taken = swapped(give_back)
    summed = (keep_own.astype(jnp.float32) + taken.astype(jnp.float32)).astype(jnp.bfloat16)
    returned = exchange(summed, 2)
    mixed = returned.reshape(EXPERTS * slot_count, D)
    gathered_rows = jnp.dot(select, mixed, preferred_element_type=jnp.float32).reshape(TOK, 2, D)
    gate_scale = jnp.where(
        kept_mask, gate_ints.reshape(-1).astype(jnp.float32) / 1024.0, 0.0
    ).reshape(TOK, 2, 1)
    expert_mix = jnp.sum(gate_scale * gathered_rows, 1).astype(jnp.bfloat16)
    return (attended, expert_mix)


def solution(mesh):
    placed = (
        P("seq", None), P("seq", None), P("seq", None), P("seq", None), P(None, "seq"), P(),
        P(None, None, "seq"), P("seq", None), P("seq", None), P("seq", None), P("seq"), P(),
    )
    return jax.shard_map(
        body, mesh=mesh, in_specs=placed, out_specs=(P("seq", None), P("seq", None)), check_vma=False
    )
```

time: 260 us -> 167 us (0.64)
  Pallas kernels: 0 us -> 113 us
  starting transfers between devices: 60.1 us -> 0.34 us
  blocking collectives: 55.5 us -> 0 us
  matrix products: 40.1 us -> 13 us
  waiting for transfers between devices: 32.2 us -> 6.13 us
  local copies, waits for them, and re-layouts: 33.2 us -> 12.7 us
  between operations: 14.8 us -> 0.96 us
    pallas_call x0 -> x3, Pallas kernels: none -> 113 us  [the longest x1 65.8 us: attend(): pl.pallas_call(attend_kernel, out_shape=(jax.ShapeDtypeStruct((TOK, D), b...]
    ppermute x18 -> x2, starting transfers between devices: 56.1 us -> 0.34 us  [swapped(): return lax.ppermute(value, 'seq', [(s, s ^ 1) for s in range(NDEV)])]
    all_to_all x1 -> x0, blocking collectives: 55.5 us -> none  [body(): lax.all_to_all(outgoing, 'seq', split_axis=0, concat_axis=0, tiled=True)]
    unnamed x65 -> x19, local copies, waits for them, and re-layouts: 27.3 us -> 1.66 us
    all_to_all x1 -> x0, waiting for transfers between devices: 21.9 us -> none  [body(): lax.all_to_all(summed, 'seq', split_axis=0, concat_axis=0, tiled=True)]
    dot_general x7 -> x2, matrix products: 29.6 us -> 10.8 us  [the longest x1 7.52 us: body(): jnp.einsum('nkd,dgf->gnkf', rows_in, expert_in, preferred_element_type=jn...]
    sub x4 -> x0, matrix products: 8.38 us -> none  [one_head(): weights_raw = jnp.exp(scores - row_max)]
    reshape x2 -> x4, local copies, waits for them, and re-layouts: 1.06 us -> 5.3 us  [the longest x1 3.19 us: body(): mixed = returned.reshape(EXPERTS * slot_count, D)]
  transfers between devices with their start and end apart: 20 -> 2, of which waited for: 4 -> 2; matrix products, arithmetic and copies ran while one was open for 14% -> 0% of each run, Pallas kernels for 0% -> 0%
where the time goes in v1:
time: 167 us
  Pallas kernels  113 us (68%)
  other arithmetic  20.7 us (12%)
  matrix products  13 us (8%)
  local copies, waits for them, and re-layouts  12.7 us (8%)
  waiting for transfers between devices  6.13 us (4%)
    pallas_call x1, Pallas kernels, attend(): pl.pallas_call(attend_kernel, out_shape=(jax.ShapeDtypeStruct((TOK, D), b...  65.8 us
    pallas_call x2, Pallas kernels, exchange(): pl.pallas_call(exchange_kernel, out_shape=jax.ShapeDtypeStruct(rows.shape...  47.4 us
    convert_element_type x1, other arithmetic, body(): (keep_own.astype(jnp.float32) + taken.astype(jnp.float32)).astype(jnp.bfl...  8.26 us
    dot_general x1, matrix products, body(): jnp.einsum('nkd,dgf->gnkf', rows_in, expert_in, preferred_element_type=jn...  7.52 us
    another operation x2, other arithmetic, body(): jnp.stack([first_half, second_half], 1).reshape(NDEV, slot_count, D)  7.22 us
    ppermute x2, waiting for transfers between devices, swapped(): return lax.ppermute(value, 'seq', [(s, s ^ 1) for s in range(NDEV)])  6.13 us
  transfers between devices with their start and end apart: 2, of which 2 were waited for; matrix products, arithmetic and copies ran while one was open for 0% of the time, Pallas kernels for 0%

profile of v1, /device:TPU:1, one launch (start us, length us, event | category | flops | bytes accessed | tf_op | source)
XLA Modules:
  0.0 167.0 jit_solution(1087006904319814584)
XLA Ops:
  0.7 0.8 broadcast_multiply_fusion.1
  1.5 0.7 broadcast_in_dim.24
  2.2 0.8 slice.35
  3.0 0.9 bitcast_bitcast_fusion.wa
  3.9 0.7 broadcast_multiply_fusion
  4.6 0.7 reshape.151.gain
  5.3 0.8 copy.60
  6.1 0.1 mul.66
  6.2 0.1 copy.57
  6.4 0.1 mul.64
  6.5 0.1 broadcast_in_dim.25
  6.6 0.2 broadcast_in_dim.26
  6.7 0.1 copy.58
  6.9 0.2 fusion.21
  7.2 0.1 copy.56
  7.3 0.1 add.46
  7.4 0.2 select_reduce_fusion
  7.7 0.1 reduce_sum.32
  7.8 0.1 copy.61
  7.9 0.1 copy.64
  8.0 0.1 add.51
  8.2 65.8 %shard_map.131 = (bf16[128,2560]{1,0:T(8,128)(2,1)S(1)}, bf16[128,2560]{1,0:T(8,128)(2,1)S(1)}) custom-call(bf16[20,16,128]{2,1,0:T(8,128)(2,1)S(1)} %bitcast_bitcast_fusion.wa, bf16[5,16,128]{2,1,0:T(8,128)(2,1)S(1)} %bitcast.70, bf16[128,2560]{1,0:T(8,128)(2,1)S(1)} %copy-done, bf16[128,512]{1,0:T(8,128)(2,1)S(1)} %copy-done.2, ...), custom_call_target="tpu_custom_call" | custom-call | tf_op jit(solution)/shard_map/pallas_call | solution.py:302
  74.0 0.7 broadcast_in_dim.29
  74.7 0.5 reshape.153
  75.3 0.7 convolution_convert_fusion.1
  75.9 1.4 reshape.154.x
  77.3 23.5 %shard_map.132 = bf16[128,2,2560]{2,1,0:T(2,128)(2,1)} custom-call(bf16[128,2,2560]{2,1,0:T(2,128)(2,1)} %reshape.154.x), custom_call_target="tpu_custom_call" | custom-call | tf_op jit(solution)/shard_map/pallas_call | solution.py:363
  100.8 0.2 collective-permute-start
  101.0 3.1 %collective-permute-done = bf16[128,2,2560]{2,1,0:T(2,128)(2,1)S(1)} collective-permute-done((bf16[128,2,2560]{2,1,0:T(2,128)(2,1)}, bf16[128,2,2560]{2,1,0:T(2,128)(2,1)S(1)}, u32[]{:S(2)}, u32[]{:S(2)}) %collective-permute-start) | collective-permute-done | bytes 1310752 | tf_op jit(solution)/shard_map/ppermute | solution.py:374
  104.1 3.5 %fusion.12 = (bf16[128,1,2,2560]{3,2,0,1:T(2,128)(2,1)S(1)}, bf16[128,1,2,2560]{3,2,0,1:T(2,128)(2,1)S(1)}) fusion(bf16[128,2,2560]{2,1,0:T(2,128)(2,1)} %shard_map.132, bf16[128,2,2560]{2,1,0:T(2,128)(2,1)S(1)} %collective-permute-done, pred[]{:T(512)S(6)} %eq.68), kind=kLoop, calls=%fused_computation.21 | loop fusion | flops 1310720 | bytes 5242881 | tf_op jit(solution)/shard_map/stack | solution.py:405
  107.6 3.7 %pad_maximum_fusion = bf16[128,2,2,2560]{3,2,0,1:T(2,128)(2,1)S(1)} fusion(bf16[128,1,2,2560]{3,2,0,1:T(2,128)(2,1)S(1)} %get-tuple-element.15, bf16[128,1,2,2560]{3,2,0,1:T(2,128)(2,1)S(1)} %get-tuple-element.14), kind=kLoop, calls=%fused_computation.6 | loop fusion | flops 1310720 | bytes 5242880 | tf_op jit(solution)/shard_map/stack | solution.py:405
  111.3 0.0 slice-start
  111.3 0.3 copy.65
  111.6 0.0 slice-start.1
  111.6 7.5 %fusion.4 = f32[2,128,4,832]{1,3,0,2:T(8,128)S(1)} fusion(bf16[128,4,2560,1]{2,0,3,1:T(8,128)(2,1)S(1)} %bitcast.72, bf16[2560,2,832]{0,2,1:T(8,128)(2,1)} %param.18), kind=kOutput, calls=%fused_computation.13 | convolution fusion | flops 4362076160 | bytes 14548992 | tf_op jit(solution)/shard_map/nkd,dgf->gnkf/dot_general | solution.py:406
  119.2 3.3 %convolution_convert_fusion = bf16[128,4,2560]{2,0,1:T(8,128)(2,1)S(1)} fusion(bf16[832,2560]{1,0:T(8,128)(2,1)S(1)} %bitcast.80, f32[2,128,4,832]{1,3,0,2:T(8,128)S(1)} %fusion.4), kind=kOutput, calls=%fused_computation.2 | convolution fusion | flops 2184904704 | bytes 10289152 | tf_op jit(solution)/shard_map/nkf,fd->nkd/dot_general | solution.py:408
  122.5 0.2 fusion.32
  122.7 0.0 copy-start.5
  122.7 3.3 %fusion.11 = bf16[128,2,2560]{2,1,0:T(2,128)(2,1)} fusion(pred[]{:T(512)S(6)} %eq.68, bf16[128,1,2,2560]{3,0,2,1:T(8,128)(2,1)S(1)} %get-tuple-element.13, bf16[128,1,2,2560]{3,0,2,1:T(8,128)(2,1)S(1)} %get-tuple-element.12), kind=kLoop, calls=%fused_computation.20 | loop fusion | flops 655360 | bytes 3932161 | tf_op jit(solution)/shard_map/jit(_where)/select_n | solution.py:411
  126.0 0.1 collective-permute-start.1
  126.1 0.1 reduce_sum.34
  126.2 0.1 copy.62
  126.3 3.0 %collective-permute-done.1 = bf16[128,2,2560]{2,1,0:T(2,128)(2,1)} collective-permute-done((bf16[128,2,2560]{2,1,0:T(2,128)(2,1)}, bf16[128,2,2560]{2,1,0:T(2,128)(2,1)}, u32[]{:S(2)}, u32[]{:S(2)}) %collective-permute-start.1) | collective-permute-done | bytes 1310752 | tf_op jit(solution)/shard_map/ppermute | solution.py:374
  129.3 8.3 %fusion.3.x = bf16[128,2,2560]{2,1,0:T(2,128)(2,1)} fusion(bf16[128,2,2560]{2,1,0:T(2,128)(2,1)} %collective-permute-done.1, pred[]{:T(512)S(6)} %eq.68, bf16[128,1,2,2560]{3,0,2,1:T(8,128)(2,1)S(1)} %get-tuple-element.13, bf16[128,1,2,2560]{3,0,2,1:T(8,128)(2,1)S(1)} %get-tuple-element.12), kind=kLoop, calls=%fused_computation.8 | loop fusion | flops 3276800 | bytes 5242881 | tf_op jit(solution)/shard_map/convert_element_type | solution.py:413
  137.6 23.9 %shard_map.133 = bf16[128,2,2560]{2,1,0:T(2,128)(2,1)} custom-call(bf16[128,2,2560]{2,1,0:T(2,128)(2,1)} %fusion.3.x), custom_call_target="tpu_custom_call" | custom-call | tf_op jit(solution)/shard_map/pallas_call | solution.py:363
  161.6 3.2 %reshape.162 = bf16[256,2560,1]{1,0,2:T(8,128)(2,1)S(1)} reshape(bf16[128,2,2560]{2,1,0:T(2,128)(2,1)} %shard_map.133) | data formatting | bytes 2621440 | tf_op jit(solution)/shard_map/reshape | solution.py:415
  164.8 1.4 fusion.9
  166.2 0.8 copy.80
  (27 shorter events, 0.2 us)
Async XLA Ops:
  0.6 7.3 %copy-start.4 = (s32[128,2]{0,1:T(2,128)S(1)}, s32[128,2]{0,1:T(2,128)}, u32[]{:S(2)}) copy-start(s32[128,2]{0,1:T(2,128)} %param.20) | copy-start | bytes 3076
  0.6 7.5 %copy-start.3 = (bf16[128,512]{1,0:T(8,128)(2,1)S(1)}, bf16[128,512]{1,0:T(8,128)(2,1)}, u32[]{:S(2)}) copy-start(bf16[128,512]{1,0:T(8,128)(2,1)} %v.1) | copy-start | bytes 393220
  0.7 7.5 %copy-start.2 = (bf16[128,512]{1,0:T(8,128)(2,1)S(1)}, bf16[128,512]{1,0:T(8,128)(2,1)}, u32[]{:S(2)}) copy-start(bf16[128,512]{1,0:T(8,128)(2,1)} %k.1) | copy-start | bytes 393220
  0.7 7.5 %copy-start = (bf16[128,2560]{1,0:T(8,128)(2,1)S(1)}, bf16[128,2560]{1,0:T(8,128)(2,1)}, u32[]{:S(2)}) copy-start(bf16[128,2560]{1,0:T(8,128)(2,1)} %q.1) | copy-start | bytes 1966084
  0.7 7.5 %copy-start.1 = (bf16[128,2560]{1,0:T(8,128)(2,1)S(1)}, bf16[128,2560]{1,0:T(8,128)(2,1)}, u32[]{:S(2)}) copy-start(bf16[128,2560]{1,0:T(8,128)(2,1)} %res.1) | copy-start | bytes 1966084
  100.8 3.3 %collective-permute-start = (bf16[128,2,2560]{2,1,0:T(2,128)(2,1)}, bf16[128,2,2560]{2,1,0:T(2,128)(2,1)S(1)}, u32[]{:S(2)}, u32[]{:S(2)}) collective-permute-start(bf16[128,2,2560]{2,1,0:T(2,128)(2,1)} %shard_map.132), channel_id=1, source_target_pairs={{0,1},{1,0},{2,3},{3,2},{4,5},{5,4},{6,7},{7,6},{8,9},{9,8},{10,11... | collective-permute-start | bytes 3932168 | tf_op jit(solution)/shard_map/ppermute | solution.py:374
  111.3 7.8 %slice-start = ((s8[4259840]{0:T(1024)(128)(4,1)}), s8[4194304]{0:T(1024)(128)(4,1)S(1)}, s32[]{:S(2)}) async-start(s8[4259840]{0:T(1024)(128)(4,1)} %bitcast.79), calls=%async_computation | async-start | bytes 8388608
  111.6 7.6 %slice-start.1 = ((s8[4259840]{0:T(1024)(128)(4,1)}), s8[65536]{0:T(1024)(128)(4,1)S(1)}, s32[]{:S(2)}) async-start(s8[4259840]{0:T(1024)(128)(4,1)} %bitcast.79), calls=%async_computation.1 | async-start | bytes 131072
  122.7 3.6 %copy-start.5 = (s32[128,2]{0,1:T(2,128)S(1)}, s32[128,2]{0,1:T(2,128)}, u32[]{:S(2)}) copy-start(s32[128,2]{0,1:T(2,128)} %param.21) | copy-start | bytes 3076
  126.0 3.4 %collective-permute-start.1 = (bf16[128,2,2560]{2,1,0:T(2,128)(2,1)}, bf16[128,2,2560]{2,1,0:T(2,128)(2,1)}, u32[]{:S(2)}, u32[]{:S(2)}) collective-permute-start(bf16[128,2,2560]{2,1,0:T(2,128)(2,1)} %fusion.11), channel_id=1, source_target_pairs={{0,1},{1,0},{2,3},{3,2},{4,5},{5,4},{6,7},{7,6},{8,9},{9,8},{10,11... | collective-permute-start | bytes 3932168 | tf_op jit(solution)/shard_map/ppermute | solution.py:374

commit v2 on v1

--- a/solution.py
+++ b/solution.py
@@ -45,29 +45,75 @@
     return tuple(idx) + (pl.ds(t0, tn),)
 
 
-def attend_kernel(
-    wa, wb, q, k, v, res, gain, att_out, norm_out,
-    G, B1, BX, Kb, Vb, bias, ctx, attp, attt,
+def order(i):
+    s = (i * 37) % NDEV
+    return [s // 32, (s // 8) % 4, (s // 2) % 4, s % 2]
+
+
+def routing(routes, gates, modal, cap, st, wt):
+    rows = 2 * NDEV
+    rho = lax.broadcasted_iota(jnp.int32, (rows, TOK), 0)
+    key, turn = jnp.right_shift(rho, 1), jnp.bitwise_and(rho, 1)
+    mod = modal[...][None, :]
+    is0 = key == routes[0:1] * 2 + mod
+    is1 = key == routes[1:2] * 2 + mod
+    hit = jnp.where(is0 | is1, 1.0, 0.0)
+    before = lax.broadcasted_iota(jnp.int32, (TOK, TOK), 0) < lax.broadcasted_iota(jnp.int32, (TOK, TOK), 1)
+    rank = jnp.dot(
+        hit.astype(jnp.bfloat16), jnp.where(before, 1.0, 0.0).astype(jnp.bfloat16),
+        preferred_element_type=jnp.float32,
+    )
+    rho_e = lax.broadcasted_iota(jnp.int32, (rows, EXPERTS), 0)
+    at_e = lax.broadcasted_iota(jnp.int32, (rows, EXPERTS), 1) == jnp.right_shift(rho_e, 2)
+    cap_e = jnp.where(jnp.bitwise_and(rho_e, 2) == 0, cap[0:1], cap[1:2]).astype(jnp.float32)
+    limit = jnp.sum(jnp.where(at_e, cap_e, 0.0), -1, keepdims=True)
+    turn_f = turn.astype(jnp.float32)
+    kept = jnp.where((rank == turn_f) & (turn_f < limit), hit, 0.0)
+    st[...] = kept.astype(jnp.bfloat16)
+    g = jnp.where(is0, gates[0:1], gates[1:2])
+    high = jnp.bitwise_and(g, 1016)
+    wt[0] = jnp.transpose(high.astype(jnp.float32) * kept).astype(jnp.bfloat16)
+    wt[1] = jnp.transpose((g - high).astype(jnp.float32) * kept).astype(jnp.bfloat16)
+
+
+def layer_kernel(
+    w, q, k, v, res, gain, w_in, w_down, routes, gates, modal, cap, att_out, mix_out,
+    G, B1, BX, Kb, Vb, bias, ctx, attp, attt, normed, st, wt, win, wdn,
+    xs, xr, xf, rows, actt, pown, psend, precv, ys, ret,
     s1, r1, s2, r2, s3, r3, s4, r4, sb1, rb1, sb2, rb2, sb3, rb3, sb4, rb4,
     kvs, kvr, cxs, cxr, ats, atr, lsem,
+    dsem, drem, dloc, fsem, frem, psem, prem, ysem, yrem, yloc,
 ):
     me = lax.axis_index("seq")
     cs = coords(me)
     y, z, x, core = cs
     bar = pltpu.get_barrier_semaphore()
     sib = dev([y, z, x, 1 - core])
-    peers = [dev(shift(cs, dim, d)) for dim in range(3) for d in DELTAS]
-    peers += [sib, lax.rem(me + 8, NDEV), lax.rem(me + NDEV - 8, NDEV)]
-    for p in peers:
-        pl.semaphore_signal(bar, inc=1, device_id=(p,), device_id_type=MESH)
+
+    def signal(i, c):
+        pl.semaphore_signal(bar, inc=1, device_id=(lax.rem(me + i, NDEV),), device_id_type=MESH)
+        return c
+
+    lax.fori_loop(1, NDEV, signal, 0)
     own = [
-        pltpu.make_async_copy(wa, G.at[y, z, x], lsem.at[0]),
-        pltpu.make_async_copy(wb, B1.at[x], lsem.at[1]),
-        pltpu.make_async_copy(k, Kb.at[8], lsem.at[2]),
-        pltpu.make_async_copy(v, Vb.at[8], lsem.at[3]),
+        pltpu.make_async_copy(k, Kb.at[8], lsem.at[0]),
+        pltpu.make_async_copy(v, Vb.at[8], lsem.at[1]),
     ]
     for c in own:
         c.start()
+    weights = [
+        pltpu.make_async_copy(w_in, win, lsem.at[2]),
+        pltpu.make_async_copy(w_down, wdn, lsem.at[3]),
+    ]
+    for c in weights:
+        c.start()
+    for t in range(KT):
+        G[y, z, x, t] = w[0:16, t * 128:(t + 1) * 128]
+    tail = w[16:20].astype(jnp.float32)
+    for i in range(5):
+        B1[x, i] = jnp.concatenate(
+            [tail[:, n * 640 + i * 128:n * 640 + i * 128 + 128] for n in range(4)], 0
+        ).astype(jnp.bfloat16)
     row = lax.broadcasted_iota(jnp.int32, (TOK, TOK), 0)
     col = lax.broadcasted_iota(jnp.int32, (TOK, TOK), 1)
     for j in range(9):
@@ -81,7 +127,7 @@
         bias[:, j * TOK:(j + 1) * TOK] = jnp.where(m, 0.0, -jnp.inf)
     for c in own:
         c.wait()
-    pl.semaphore_wait(bar, len(peers))
+    pl.semaphore_wait(bar, NDEV - 1)
     sends = []
 
     def rc(src, dst, ss, rs, dv):
@@ -197,6 +243,7 @@
                     rl.append(rc(b_, b_, sb4.at[i, n], rb4.at[i, n], dev(shift(cs, 0, dto))))
 
     relay(0)
+    routing(routes, gates, modal, cap, st, wt)
     kvd = []
     for p_ in kvx:
         for n in range(2):
@@ -287,22 +334,133 @@
     for t in range(KT):
         ls = slice(t * 128, (t + 1) * 128)
         hd = res[:, ls].astype(jnp.float32) + att_out[:, ls].astype(jnp.float32)
-        norm_out[:, ls] = (hd * inv * gain[:, ls]).astype(jnp.bfloat16)
+        normed[:, ls] = (hd * inv * gain[ls][None, :]).astype(jnp.bfloat16)
+
+    xs[...] = jnp.dot(st[...], normed[...], preferred_element_type=jnp.float32).astype(
+        jnp.bfloat16
+    ).reshape(NDEV, CAP, D)
+    mine = pltpu.make_async_copy(xs.at[me], xr.at[0], dloc)
+    mine.start()
+    HALF = NDEV // 2
+
+    def offset(i, sign):
+        off = order(i)
+        full = [4, 4, 4, 2]
+        return dev([lax.rem(cs[n] + (off[n] if sign > 0 else full[n] - off[n]), full[n]) for n in range(4)])
+
+    def send_half(half):
+        def send(i, c):
+            t = offset(i, 1)
+            pltpu.make_async_remote_copy(
+                src_ref=xs.at[t], dst_ref=xr.at[i], send_sem=dsem.at[half], recv_sem=drem.at[half],
+                device_id=(t,), device_id_type=MESH,
+            ).start()
+            return c
+
+        lax.fori_loop(max(1, half * HALF), (half + 1) * HALF, send, 0)
+
+    send_half(0)
+    send_half(1)
+    mine.wait()
+
+    def whole(src, dst, half, ss, rs):
+        n = HALF - 1 if half == 0 else HALF
+        part = pl.ds(half * HALF, n)
+        return pltpu.make_async_remote_copy(
+            src_ref=src.at[part], dst_ref=dst.at[part], send_sem=ss.at[half], recv_sem=rs.at[half],
+            device_id=(sib,), device_id_type=MESH,
+        )
+
+    for c in weights:
+        c.wait()
+    fwd, back = [], []
+
+    def arrive(half):
+        whole(xs, xr, half, dsem, drem).wait_recv()
+        part = pl.ds(half * HALF, HALF)
+        fwd.append(rc(xr.at[part], xf.at[part], fsem.at[half], frem.at[half], sib))
+        rows[:TOK] = xr[part].reshape(TOK, D)
+        fwd[half].wait_recv()
+        rows[TOK:] = xf[part].reshape(TOK, D)
+
+    def experts(half):
+        def hidden(n, c):
+            at = pl.ds(pl.multiple_of(n * 208, 16), 208)
+            nt = (((1,), (1,)), ((), ()))
+            gate = lax.dot_general(win[0, at], rows[...], nt, preferred_element_type=jnp.float32)
+            up = lax.dot_general(win[1, at], rows[...], nt, preferred_element_type=jnp.float32)
+            actt[at] = (gate * lax.logistic(gate) * up).astype(jnp.bfloat16)
+            return c
+
+        lax.fori_loop(0, 4, hidden, 0)
+        act = jnp.transpose(actt[...].astype(jnp.float32)).astype(jnp.bfloat16)
+        for n in range(2):
+            ls = pl.ds(n * 1280, 1280)
+            psend[half, :, ls] = jnp.dot(
+                act[TOK:], wdn[:, ls], preferred_element_type=jnp.float32
+            ).astype(jnp.bfloat16)
+        back.append(rc(psend.at[half], precv.at[half], psem.at[half], prem.at[half], sib))
+        for n in range(2):
+            ls = pl.ds(n * 1280, 1280)
+            pown[:, ls] = jnp.dot(
+                act[:TOK], wdn[:, ls], preferred_element_type=jnp.float32
+            ).astype(jnp.bfloat16)
+
+    def give(half):
+        back[half].wait_recv()
+        part = pl.ds(half * HALF, HALF)
+        ys[part] = (
+            pown[...].astype(jnp.float32) + precv[half].astype(jnp.float32)
+        ).astype(jnp.bfloat16).reshape(HALF, CAP, D)
+
+        def send(i, c):
+            t = offset(i, -1)
+            pltpu.make_async_remote_copy(
+                src_ref=ys.at[i], dst_ref=ret.at[me], send_sem=ysem.at[half], recv_sem=yrem.at[0],
+                device_id=(t,), device_id_type=MESH,
+            ).start()
+            return c
+
+        lax.fori_loop(max(1, half * HALF), (half + 1) * HALF, send, 0)
+
+    arrive(0)
+    experts(0)
+    give(0)
+    home = pltpu.make_async_copy(ys.at[0], ret.at[me], yloc)
+    home.start()
+    arrive(1)
+    experts(1)
+    give(1)
+    home.wait()
+    for half in range(2):
+        whole(xs, xr, half, dsem, drem).wait_send()
+        whole(ys, ret, half, ysem, ysem).wait_send()
+    every = pl.ds(0, NDEV - 1)
+    pltpu.make_async_remote_copy(
+        src_ref=ys.at[every], dst_ref=ret.at[every], send_sem=ysem.at[0], recv_sem=yrem.at[0],
+        device_id=(sib,), device_id_type=MESH,
+    ).wait_recv()
+    back_rows = ret[...].reshape(2 * NDEV, D)
+    mix = jnp.dot(wt[0], back_rows, preferred_element_type=jnp.float32) + jnp.dot(
+        wt[1], back_rows, preferred_element_type=jnp.float32
+    )
+    mix_out[...] = (mix * (1.0 / 1024.0)).astype(jnp.bfloat16)
     for c in sends:
         c.wait_send()
 
 
-def attend(residual, queries, keys, values, out_proj, norm_gain):
-    wt = out_proj.T
-    wa = wt[:16].reshape(16, KT, 128).transpose(1, 0, 2)
-    wb = wt[16:].reshape(4, 4, 5, 128).transpose(2, 1, 0, 3).reshape(5, 16, 128)
+def body(
+    residual, queries, keys, values, out_proj, norm_gain, expert_in, expert_down,
+    routes, gate_ints, modality, capacity,
+):
     any_ = pl.BlockSpec(memory_space=pl.ANY)
     vm = pl.BlockSpec(memory_space=pltpu.VMEM)
     bf = jnp.bfloat16
+    cols = expert_in.shape[2]
     return pl.pallas_call(
-        attend_kernel,
+        layer_kernel,
         out_shape=(jax.ShapeDtypeStruct((TOK, D), bf), jax.ShapeDtypeStruct((TOK, D), bf)),
-        in_specs=[any_, any_, vm, any_, any_, vm, vm],
+        in_specs=[vm, vm, any_, any_, vm, vm, any_, any_, vm, vm, vm, vm],
         out_specs=(vm, vm),
         scratch_shapes=[
             pltpu.VMEM((4, 4, 4, KT, 16, 128), bf),
@@ -314,111 +472,35 @@
             pltpu.VMEM((2, KV_HEADS, TOK, GROUP * HEAD), bf),
             pltpu.VMEM((2, 2, 1280, TOK), bf),
             pltpu.VMEM((D, TOK), jnp.float32),
+            pltpu.VMEM((TOK, D), bf),
+            pltpu.VMEM((2 * NDEV, TOK), bf),
+            pltpu.VMEM((2, TOK, 2 * NDEV), bf),
+            pltpu.VMEM((2, cols, D), bf),
+            pltpu.VMEM((cols, D), bf),
+            pltpu.VMEM((NDEV, CAP, D), bf),
+            pltpu.VMEM((NDEV, CAP, D), bf),
+            pltpu.VMEM((NDEV, CAP, D), bf),
+            pltpu.VMEM((2 * TOK, D), bf),
+            pltpu.VMEM((cols, 2 * TOK), bf),
+            pltpu.VMEM((TOK, D), bf),
+            pltpu.VMEM((2, TOK, D), bf),
+            pltpu.VMEM((2, TOK, D), bf),
+            pltpu.VMEM((NDEV, CAP, D), bf),
+            pltpu.VMEM((NDEV, CAP, D), bf),
             DMA((3, 3)), DMA((3, 3)), DMA((3, 3)), DMA((3, 3)),
             DMA((3, 4, 2)), DMA((3, 4, 2)), DMA((3, 4, 2)), DMA((3, 4, 2)),
             DMA((3,)), DMA((3,)), DMA((3,)), DMA((3,)),
             DMA((4, 2)), DMA((4, 2)), DMA((4, 2)), DMA((4, 2)),
             DMA((2, 8)), DMA((2, 8)), DMA((4,)), DMA((4,)), DMA, DMA, DMA((4,)),
+            DMA((2,)), DMA((2,)), DMA, DMA((2,)), DMA((2,)), DMA((2,)), DMA((2,)), DMA((2,)), DMA((1,)), DMA,
         ],
         compiler_params=pltpu.CompilerParams(
-            has_side_effects=True, collective_id=0, vmem_limit_bytes=48 * 2**20
+            has_side_effects=True, collective_id=0, vmem_limit_bytes=60 * 2**20
         ),
-    )(wa, wb, queries, keys, values, residual, norm_gain.reshape(1, D))
-
-
-def exchange_kernel(x, o, ssem, rsem, lsem):
-    me = lax.axis_index("seq")
-    bar = pltpu.get_barrier_semaphore()
-
-    def signal(s, c):
-        pl.semaphore_signal(bar, inc=1, device_id=(lax.rem(me + s, NDEV),), device_id_type=MESH)
-        return c
-
-    lax.fori_loop(1, NDEV, signal, 0)
-    pl.semaphore_wait(bar, NDEV - 1)
-    own = pltpu.make_async_copy(x.at[me], o.at[me], lsem)
-    own.start()
-    cs = coords(me)
-
-    def send(i, c):
-        s = (i * 37) % NDEV
-        t = dev([(cs[0] + s // 32) % 4, (cs[1] + (s // 8) % 4) % 4, (cs[2] + (s // 2) % 4) % 4, (cs[3] + s % 2) % 2])
-        pltpu.make_async_remote_copy(
-            src_ref=x.at[t], dst_ref=o.at[me], send_sem=ssem, recv_sem=rsem, device_id=(t,), device_id_type=MESH
-        ).start()
-        return c
-
-    lax.fori_loop(1, NDEV, send, 0)
-    own.wait()
-    whole = pl.ds(0, NDEV - 1)
-    done = pltpu.make_async_remote_copy(
-        src_ref=x.at[whole], dst_ref=o.at[whole], send_sem=ssem, recv_sem=rsem,
-        device_id=(lax.rem(me + 1, NDEV),), device_id_type=MESH,
+    )(
+        out_proj.T, queries, keys, values, residual, norm_gain, expert_in.transpose(1, 2, 0), expert_down,
+        routes.T, gate_ints.T, modality, capacity.T,
     )
-    done.wait_send()
-    done.wait_recv()
-
-
-def exchange(rows, cid):
-    return pl.pallas_call(
-        exchange_kernel,
-        out_shape=jax.ShapeDtypeStruct(rows.shape, rows.dtype),
-        in_specs=[pl.BlockSpec(memory_space=pl.ANY)],
-        out_specs=pl.BlockSpec(memory_space=pl.ANY),
-        scratch_shapes=[DMA, DMA, DMA],
-        compiler_params=pltpu.CompilerParams(has_side_effects=True, collective_id=cid),
-    )(rows)
-
-
-def swapped(value):
-    return lax.ppermute(value, "seq", [(s, s ^ 1) for s in range(NDEV)])
-
-
-def body(
-    residual, queries, keys, values, out_proj, norm_gain, expert_in, expert_down,
-    routes, gate_ints, modality, capacity,
-):
-    device_pos = lax.axis_index("seq")
-    attended, normed = attend(residual, queries, keys, values, out_proj, norm_gain)
-    slot_count = 2 * CAP
-    chosen = routes.reshape(-1)
-    modal_flag = jnp.repeat(modality, 2)
-    slot_key = chosen * 2 + modal_flag
-    onehot = (slot_key[:, None] == jnp.arange(2 * EXPERTS, dtype=jnp.int32)[None, :]).astype(jnp.int32)
-    rank_in = jnp.sum((jnp.cumsum(onehot, 0) - onehot) * onehot, 1)
-    limit_of = jnp.sum(onehot * capacity.reshape(1, -1), 1)
-    kept_mask = rank_in < limit_of
-    column = chosen * slot_count + modal_flag * CAP + rank_in
-    select = (
-        (column[:, None] == jnp.arange(EXPERTS * slot_count, dtype=jnp.int32)[None, :]) & kept_mask[:, None]
-    ).astype(jnp.bfloat16)
-    doubled = jnp.repeat(normed, 2, axis=0)
-    slot_table = lax.dot_general(
-        select, doubled, (((0,), (0,)), ((), ())), preferred_element_type=jnp.float32
-    ).astype(jnp.bfloat16)
-    hidden_each = expert_in.shape[2]
-    own_rows = exchange(slot_table.reshape(NDEV, CAP, D), 1)
-    partner = swapped(own_rows)
-    is_lower = device_pos % 2 == 0
-    first_half = jnp.where(is_lower, own_rows, partner)
-    second_half = jnp.where(is_lower, partner, own_rows)
-    rows_in = jnp.stack([first_half, second_half], 1).reshape(NDEV, slot_count, D)
-    gate_up = jnp.einsum("nkd,dgf->gnkf", rows_in, expert_in, preferred_element_type=jnp.float32)
-    active = (jax.nn.silu(gate_up[0]) * gate_up[1]).astype(jnp.bfloat16)
-    partial_value = jnp.einsum("nkf,fd->nkd", active, expert_down, preferred_element_type=jnp.float32)
-    partial_value = lax.optimization_barrier(partial_value.astype(jnp.bfloat16)).reshape(NDEV, 2, CAP, D)
-    keep_own = jnp.where(is_lower, partial_value[:, 0], partial_value[:, 1])
-    give_back = jnp.where(is_lower, partial_value[:, 1], partial_value[:, 0])
-    taken = swapped(give_back)
-    summed = (keep_own.astype(jnp.float32) + taken.astype(jnp.float32)).astype(jnp.bfloat16)
-    returned = exchange(summed, 2)
-    mixed = returned.reshape(EXPERTS * slot_count, D)
-    gathered_rows = jnp.dot(select, mixed, preferred_element_type=jnp.float32).reshape(TOK, 2, D)
-    gate_scale = jnp.where(
-        kept_mask, gate_ints.reshape(-1).astype(jnp.float32) / 1024.0, 0.0
-    ).reshape(TOK, 2, 1)
-    expert_mix = jnp.sum(gate_scale * gathered_rows, 1).astype(jnp.bfloat16)
-    return (attended, expert_mix)
 
 
 def solution(mesh):

time: 167 us -> 121 us (0.72)
  other arithmetic: 20.7 us -> 0 us
  matrix products: 13 us -> 0 us
  local copies, waits for them, and re-layouts: 12.7 us -> 3.93 us
  waiting for transfers between devices: 6.13 us -> 0 us
  Pallas kernels: 113 us -> 116 us
    dot_general x4 -> x0, matrix products: 13 us -> none  [the longest x1 7.52 us: body(): jnp.einsum('nkd,dgf->gnkf', rows_in, expert_in, preferred_element_type=jn...]
    convert_element_type x1 -> x0, other arithmetic: 8.26 us -> none  [body(): (keep_own.astype(jnp.float32) + taken.astype(jnp.float32)).astype(jnp.bfl...]
    another operation x5 -> x0, other arithmetic: 7.47 us -> none  [the longest x2 7.22 us: body(): jnp.stack([first_half, second_half], 1).reshape(NDEV, slot_count, D)]
    ppermute x2 -> x0, waiting for transfers between devices: 6.13 us -> none  [swapped(): return lax.ppermute(value, 'seq', [(s, s ^ 1) for s in range(NDEV)])]
    reshape x5 -> x0, local copies, waits for them, and re-layouts: 5.83 us -> none  [the longest x1 3.19 us: body(): mixed = returned.reshape(EXPERTS * slot_count, D)]
    select_n x2 -> x0, other arithmetic: 3.28 us -> none  [the longest x1 3.25 us: body(): give_back = jnp.where(is_lower, partial_value[:, 1], partial_value[:, 0])]
    pallas_call x3 -> x1, Pallas kernels: 113 us -> 116 us  [body(): pl.pallas_call(layer_kernel, out_shape=(jax.ShapeDtypeStruct((TOK, D), bf...]
    unnamed x19 -> x2, local copies, waits for them, and re-layouts: 1.66 us -> 3.93 us
  transfers between devices with their start and end apart: 2 -> 0, of which waited for: 2 -> 0; matrix products, arithmetic and copies ran while one was open for 0% -> 0% of each run, Pallas kernels for 0% -> 0%
where the time goes in v2:
time: 121 us; the launch traced here: 120 us
  Pallas kernels  116 us (96%)
  local copies, waits for them, and re-layouts  3.93 us (3%)
    pallas_call x1, Pallas kernels, body(): pl.pallas_call(layer_kernel, out_shape=(jax.ShapeDtypeStruct((TOK, D), bf...  116 us
    unnamed x2, local copies, waits for them, and re-layouts  3.93 us

profile of v2, /device:TPU:1, one launch (start us, length us, event | category | flops | bytes accessed | tf_op | source)
XLA Modules:
  0.0 120.4 jit_solution(14078621192469410033)
XLA Ops:
  0.6 115.8 %shard_map.131 = (bf16[128,2560]{1,0:T(8,128)(2,1)}, bf16[128,2560]{1,0:T(8,128)(2,1)}) custom-call(bf16[20,2560]{1,0:T(8,128)(2,1)} %bitcast.6, bf16[128,2560]{1,0:T(8,128)(2,1)} %q.1, bf16[128,512]{1,0:T(8,128)(2,1)} %k.1, bf16[128,512]{1,0:T(8,128)(2,1)} %v.1, bf16[128,2560]{1,0:T(8,128)(2,1)} %res.1, f32[2560]{0:T(1024)} %gain.1, ...), custom_call_target="tpu_custom_call" | custom-call | tf_op jit(solution)/shard_map/pallas_call | solution.py:460
  116.4 2.0 %copy.16 = bf16[128,2560]{1,0:T(8,128)(2,1)} copy(bf16[128,2560]{1,0:T(8,128)(2,1)} %get-tuple-element.4) | data formatting | bytes 1310720
  118.4 2.0 %copy.17 = bf16[128,2560]{1,0:T(8,128)(2,1)} copy(bf16[128,2560]{1,0:T(8,128)(2,1)} %get-tuple-element.5) | data formatting | bytes 1310720

commit v3 on v2

--- a/solution.py
+++ b/solution.py
@@ -20,7 +20,7 @@
 MESH = pl.DeviceIdType.MESH
 DMA = pltpu.SemaphoreType.DMA
 DELTAS = (1, 3, 2)
-PARTS = (((2, 1, 0), 0, 7), ((1, 0, 2), 7, 5), ((0, 2, 1), 12, 8))
+PARTS = (((2, 1, 0), 0, 5), ((1, 0, 2), 5, 6), ((2, 0, 1), 11, 9))
 KT = D // 128
 
 
@@ -78,10 +78,10 @@
 
 def layer_kernel(
     w, q, k, v, res, gain, w_in, w_down, routes, gates, modal, cap, att_out, mix_out,
-    G, B1, BX, Kb, Vb, bias, ctx, attp, attt, normed, st, wt, win, wdn,
+    G, B1, BX, Ko, Vo, Kb, Vb, qb, bias, ctx, attp, attt, normed, st, wt, win, wdn,
     xs, xr, xf, rows, actt, pown, psend, precv, ys, ret,
     s1, r1, s2, r2, s3, r3, s4, r4, sb1, rb1, sb2, rb2, sb3, rb3, sb4, rb4,
-    kvs, kvr, cxs, cxr, ats, atr, lsem,
+    kzs, kzr, kxs, kxr, kds, kdr, cxs, cxr, ats, atr, lsem,
     dsem, drem, dloc, fsem, frem, psem, prem, ysem, yrem, yloc,
 ):
     me = lax.axis_index("seq")
@@ -95,15 +95,19 @@
         return c
 
     lax.fori_loop(1, NDEV, signal, 0)
-    own = [
-        pltpu.make_async_copy(k, Kb.at[8], lsem.at[0]),
-        pltpu.make_async_copy(v, Vb.at[8], lsem.at[1]),
-    ]
+    half_w = KV_HEADS * HEAD // 2
+    own = []
+    for n, (src, own_, buf) in enumerate(((k, Ko, Kb), (v, Vo, Vb))):
+        for hf in range(2):
+            own.append(pltpu.make_async_copy(src.at[:, pl.ds(hf * half_w, half_w)], own_.at[hf], lsem.at[3 * n + hf]))
+        own.append(pltpu.make_async_copy(
+            src.at[:, pl.ds(pl.multiple_of(core * half_w, half_w), half_w)], buf.at[8 + core], lsem.at[3 * n + 2]
+        ))
     for c in own:
         c.start()
     weights = [
-        pltpu.make_async_copy(w_in, win, lsem.at[2]),
-        pltpu.make_async_copy(w_down, wdn, lsem.at[3]),
+        pltpu.make_async_copy(w_in, win, lsem.at[6]),
+        pltpu.make_async_copy(w_down, wdn, lsem.at[7]),
     ]
     for c in weights:
         c.start()
@@ -116,15 +120,18 @@
         ).astype(jnp.bfloat16)
     row = lax.broadcasted_iota(jnp.int32, (TOK, TOK), 0)
     col = lax.broadcasted_iota(jnp.int32, (TOK, TOK), 1)
-    for j in range(9):
-        ok = me - 8 + j >= 0
-        if j == 0:
-            m = (col > row) & ok
-        elif j == 8:
-            m = col <= row
-        else:
-            m = (col >= 0) & ok
-        bias[:, j * TOK:(j + 1) * TOK] = jnp.where(m, 0.0, -jnp.inf)
+    for p in range(2):
+        for j in range(9):
+            ok = me - core - 8 + j + p >= 0
+            if j == 0:
+                m = (col > row) & ok
+            elif j == 8:
+                m = col <= row
+            else:
+                m = (col >= 0) & ok
+            bias[p, :, j * TOK:(j + 1) * TOK] = jnp.where(m, 0.0, -jnp.inf)
+    mine_q = pl.ds(pl.multiple_of(core * (D // 2), 128), D // 2)
+    qb[core] = q[:, mine_q]
     for c in own:
         c.wait()
     pl.semaphore_wait(bar, NDEV - 1)
@@ -138,30 +145,6 @@
         sends.append(c)
         return c
 
-    nxt = lax.rem(me + 8, NDEV)
-    kv4 = [rc(b_.at[8], b_.at[0], kvs.at[n, 3], kvr.at[n, 3], nxt) for n, b_ in enumerate((Kb, Vb))]
-    kvx = []
-    for dlt in (1, 2, 3):
-        tgt = dev(shift(cs, 2, dlt))
-        pair = []
-        for n, b_ in enumerate((Kb, Vb)):
-            pair.append(
-                tuple(
-                    pltpu.make_async_remote_copy(
-                        src_ref=b_.at[s], dst_ref=b_.at[8 - 2 * dlt], send_sem=kvs.at[n, dlt - 1],
-                        recv_sem=kvr.at[n, dlt - 1], device_id=(tgt,), device_id_type=MESH,
-                    )
-                    for s in (8, 0)
-                )
-            )
-        kvx.append(pair)
-        sends += [p_[0] for p_ in pair]
-
-        @pl.when(x + dlt < 4)
-        def _():
-            for p_ in pair:
-                p_[0].start()
-
     p1 = []
     for pi, ((a, bb, c), t0, tn) in enumerate(PARTS):
         sl = wslice(cs, (), {}, t0, tn)
@@ -169,6 +152,42 @@
             [rc(G.at[sl], G.at[sl], s1.at[pi, i], r1.at[pi, i], dev(shift(cs, a, d))) for i, d in enumerate(DELTAS)]
         )
     pb1 = [rc(B1.at[x], B1.at[x], sb1.at[i], rb1.at[i], dev(shift(cs, 2, d))) for i, d in enumerate(DELTAS)]
+
+    def twin(cs_, c_):
+        return dev(cs_[:3] + [c_])
+
+    kvz, kvx, kvx_wait = [], [], []
+    up = lax.rem(me - core + 8, NDEV)
+    for n, (own_, buf) in enumerate(((Ko, Kb), (Vo, Vb))):
+        for hf in range(2):
+            kvz.append(rc(own_.at[hf], buf.at[core], kzs.at[n, hf], kzr.at[n, core], up + hf))
+    qx = rc(q.at[:, pl.ds(pl.multiple_of((1 - core) * (D // 2), 128), D // 2)], qb.at[core], cxs.at[4], cxr.at[4], sib)
+    kvd = [
+        rc(own_.at[1 - core], buf.at[8 + core], kds.at[n], kdr.at[n], sib)
+        for n, (own_, buf) in enumerate(((Ko, Kb), (Vo, Vb)))
+    ]
+    for dlt in (1, 3, 2):
+        tgt = shift(cs, 2, dlt)
+        for n, (own_, buf) in enumerate(((Ko, Kb), (Vo, Vb))):
+            for hf in range(2):
+                slot = (4 - dlt) * 2
+                fresh = pltpu.make_async_remote_copy(
+                    src_ref=own_.at[hf], dst_ref=buf.at[slot + core], send_sem=kxs.at[n, dlt - 1, hf],
+                    recv_sem=kxr.at[n, dlt - 1, core], device_id=(twin(tgt, hf),), device_id_type=MESH,
+                )
+                older = pltpu.make_async_remote_copy(
+                    src_ref=buf.at[hf], dst_ref=buf.at[slot + hf], send_sem=kxs.at[n, dlt - 1, hf],
+                    recv_sem=kxr.at[n, dlt - 1, hf], device_id=(twin(tgt, core),), device_id_type=MESH,
+                )
+                kvx.append((n, dlt, fresh, older))
+                kvx_wait.append(older)
+
+    for n, dlt, fresh, older in kvx:
+        sends.append(older)
+
+        @pl.when(x + dlt < 4)
+        def _():
+            fresh.start()
 
     p3 = [[None] * 4 for _ in PARTS]
     pb3 = [None] * 4
@@ -186,9 +205,10 @@
                 for n, d in enumerate(DELTAS[:2])
             ]
 
-    p2 = []
+    p2 = [None] * 3
     pb2 = []
-    for pi, ((a, bb, c), t0, tn) in enumerate(PARTS):
+    for pi in (0, 2, 1):
+        (a, bb, c), t0, tn = PARTS[pi]
         for n in range(3):
             p1[pi][n].wait_recv()
         if pi == 0:
@@ -201,9 +221,9 @@
                         [src[xx][i][kq * 4:kq * 4 + 4] for xx in range(4)], 0
                     ).astype(jnp.bfloat16)
         sl = wslice(cs, (a,), {}, t0, tn)
-        p2.append(
-            [rc(G.at[sl], G.at[sl], s2.at[pi, i], r2.at[pi, i], dev(shift(cs, bb, d))) for i, d in enumerate(DELTAS)]
-        )
+        p2[pi] = [
+            rc(G.at[sl], G.at[sl], s2.at[pi, i], r2.at[pi, i], dev(shift(cs, bb, d))) for i, d in enumerate(DELTAS)
+        ]
         if pi == 0:
             pb2 = [
                 rc(BX.at[y, z], BX.at[y, z], sb2.at[i], rb2.at[i], dev(shift(cs, 1, d)))
@@ -211,14 +231,18 @@
             ]
         chunk_send(pi, 0, cs[bb])
 
-    for c in kv4:
-        c.wait_recv()
-    for dlt in (1, 2, 3):
-
-        @pl.when(x + dlt >= 4)
-        def _():
-            for p_ in kvx[dlt - 1]:
-                p_[1].start()
+    for n, buf in enumerate((Kb, Vb)):
+        for hf in range(2):
+            pltpu.make_async_remote_copy(
+                src_ref=buf.at[hf], dst_ref=buf.at[hf], send_sem=kzs.at[n, hf], recv_sem=kzr.at[n, hf],
+                device_id=(up,), device_id_type=MESH,
+            ).wait_recv()
+        for n_, dlt, fresh, older in kvx:
+            if n_ == n:
+
+                @pl.when(x + dlt >= 4)
+                def _():
+                    older.start()
 
     for i, d in enumerate(DELTAS):
         for pi, ((a, bb, c), t0, tn) in enumerate(PARTS):
@@ -244,37 +268,32 @@
 
     relay(0)
     routing(routes, gates, modal, cap, st, wt)
-    kvd = []
-    for p_ in kvx:
-        for n in range(2):
-            p_[n][0].wait_recv()
-    for i in range(4):
-        src = 8 - 2 * i - 2 * core
-        for n, b_ in enumerate((Kb, Vb)):
-            kvd.append(rc(b_.at[src], b_.at[7 - 2 * i], kvs.at[n, 4 + i], kvr.at[n, 4 + i], sib))
     relay(1)
-    for c in kvd:
+    for c in kvd + kvx_wait:
         c.wait_recv()
+    qx.wait_recv()
 
     scale = HEAD ** (-0.5)
     cxc = []
-    for h in range(KV_HEADS):
-        hs = slice(h * HEAD, (h + 1) * HEAD)
-        kh = Kb[:, :, hs].reshape(9 * TOK, HEAD)
-        vh = Vb[:, :, hs].reshape(9 * TOK, HEAD)
-        for g in range(GROUP):
-            qs = slice((h * GROUP + g) * HEAD, (h * GROUP + g + 1) * HEAD)
-            s = lax.dot_general(
-                q[:, qs], kh, (((1,), (1,)), ((), ())), preferred_element_type=jnp.float32
-            ) * scale + bias[...]
-            mx = jnp.max(s, -1, keepdims=True)
-            e = jnp.exp(s - mx)
-            tot = jnp.sum(e, -1, keepdims=True)
-            o = jnp.dot(e.astype(jnp.bfloat16), vh, preferred_element_type=jnp.float32)
-            ctx[core, h, :, g * HEAD:(g + 1) * HEAD] = (o / tot).astype(jnp.bfloat16)
-        cxc.append(rc(ctx.at[core, h], ctx.at[core, h], cxs.at[h], cxr.at[h], sib))
-        if h < 2:
-            relay(h + 2)
+    for hl in range(2):
+        hs = slice(hl * HEAD, (hl + 1) * HEAD)
+        h = 2 * core + hl
+        for p in range(2):
+            kh = Kb[p:p + 9, :, hs].reshape(9 * TOK, HEAD)
+            vh = Vb[p:p + 9, :, hs].reshape(9 * TOK, HEAD)
+            for g in range(GROUP):
+                qs = slice((hl * GROUP + g) * HEAD, (hl * GROUP + g + 1) * HEAD)
+                s = lax.dot_general(
+                    qb[p, :, qs], kh, (((1,), (1,)), ((), ())), preferred_element_type=jnp.float32
+                ) * scale + bias[p]
+                mx = jnp.max(s, -1, keepdims=True)
+                e = jnp.exp(s - mx)
+                tot = jnp.sum(e, -1, keepdims=True)
+                o = jnp.dot(e.astype(jnp.bfloat16), vh, preferred_element_type=jnp.float32)
+                ctx[p, h, :, g * HEAD:(g + 1) * HEAD] = (o / tot).astype(jnp.bfloat16)
+            cxc.append(rc(ctx.at[p, h], ctx.at[p, h], cxs.at[2 * hl + p], cxr.at[2 * hl + p], sib))
+            if p == 1:
+                relay(hl + 2)
     for c in cxc:
         c.wait_recv()
     for c in rl:
@@ -449,6 +468,14 @@
         c.wait_send()
 
 
+def out_kernel(a, b, a_out, b_out, sem):
+    copies = [pltpu.make_async_copy(a, a_out, sem.at[0]), pltpu.make_async_copy(b, b_out, sem.at[1])]
+    for c in copies:
+        c.start()
+    for c in copies:
+        c.wait()
+
+
 def body(
     residual, queries, keys, values, out_proj, norm_gain, expert_in, expert_down,
     routes, gate_ints, modality, capacity,
@@ -457,7 +484,7 @@
     vm = pl.BlockSpec(memory_space=pltpu.VMEM)
     bf = jnp.bfloat16
     cols = expert_in.shape[2]
-    return pl.pallas_call(
+    outs = pl.pallas_call(
         layer_kernel,
         out_shape=(jax.ShapeDtypeStruct((TOK, D), bf), jax.ShapeDtypeStruct((TOK, D), bf)),
         in_specs=[vm, vm, any_, any_, vm, vm, any_, any_, vm, vm, vm, vm],
@@ -466,9 +493,12 @@
             pltpu.VMEM((4, 4, 4, KT, 16, 128), bf),
             pltpu.VMEM((4, 5, 16, 128), bf),
             pltpu.VMEM((4, 4, KT, 16, 128), bf),
-            pltpu.VMEM((9, TOK, KV_HEADS * HEAD), bf),
-            pltpu.VMEM((9, TOK, KV_HEADS * HEAD), bf),
-            pltpu.VMEM((TOK, 9 * TOK), jnp.float32),
+            pltpu.VMEM((2, TOK, KV_HEADS * HEAD // 2), bf),
+            pltpu.VMEM((2, TOK, KV_HEADS * HEAD // 2), bf),
+            pltpu.VMEM((10, TOK, KV_HEADS * HEAD // 2), bf),
+            pltpu.VMEM((10, TOK, KV_HEADS * HEAD // 2), bf),
+            pltpu.VMEM((2, TOK, D // 2), bf),
+            pltpu.VMEM((2, TOK, 9 * TOK), jnp.float32),
             pltpu.VMEM((2, KV_HEADS, TOK, GROUP * HEAD), bf),
             pltpu.VMEM((2, 2, 1280, TOK), bf),
             pltpu.VMEM((D, TOK), jnp.float32),
@@ -491,7 +521,8 @@
             DMA((3, 4, 2)), DMA((3, 4, 2)), DMA((3, 4, 2)), DMA((3, 4, 2)),
             DMA((3,)), DMA((3,)), DMA((3,)), DMA((3,)),
             DMA((4, 2)), DMA((4, 2)), DMA((4, 2)), DMA((4, 2)),
-            DMA((2, 8)), DMA((2, 8)), DMA((4,)), DMA((4,)), DMA, DMA, DMA((4,)),
+            DMA((2, 2)), DMA((2, 2)), DMA((2, 3, 2)), DMA((2, 3, 2)), DMA((2,)), DMA((2,)),
+            DMA((5,)), DMA((5,)), DMA, DMA, DMA((8,)),
             DMA((2,)), DMA((2,)), DMA, DMA((2,)), DMA((2,)), DMA((2,)), DMA((2,)), DMA((2,)), DMA((1,)), DMA,
         ],
         compiler_params=pltpu.CompilerParams(
@@ -501,6 +532,11 @@
         out_proj.T, queries, keys, values, residual, norm_gain, expert_in.transpose(1, 2, 0), expert_down,
         routes.T, gate_ints.T, modality, capacity.T,
     )
+    shape = jax.ShapeDtypeStruct((TOK, D), bf)
+    return pl.pallas_call(
+        out_kernel, out_shape=(shape, shape), in_specs=[vm, vm], out_specs=(any_, any_), scratch_shapes=[DMA((2,))],
+        compiler_params=pltpu.CompilerParams(vmem_limit_bytes=4 * 2**20),
+    )(*outs)
 
 
 def solution(mesh):

time: 121 us -> 113 us (0.934)
  Pallas kernels: 116 us -> 110 us
  local copies, waits for them, and re-layouts: 3.93 us -> 2.17 us
    pallas_call x1, Pallas kernels: 116 us -> 109 us  [body(): pl.pallas_call(layer_kernel, out_shape=(jax.ShapeDtypeStruct((TOK, D), bf...]
    unnamed x2 -> x4, local copies, waits for them, and re-layouts: 3.93 us -> 2.17 us
where the time goes in v3:
time: 113 us
  Pallas kernels  110 us (97%)
  local copies, waits for them, and re-layouts  2.17 us (2%)
    pallas_call x1, Pallas kernels, body(): pl.pallas_call(layer_kernel, out_shape=(jax.ShapeDtypeStruct((TOK, D), bf...  109 us

profile of v3, /device:TPU:1, one launch (start us, length us, event | category | flops | bytes accessed | tf_op | source)
XLA Modules:
  0.0 112.7 jit_solution(7694822837421379033)
XLA Ops:
  0.6 108.6 %shard_map.131 = (bf16[128,2560]{1,0:T(8,128)(2,1)}, bf16[128,2560]{1,0:T(8,128)(2,1)}) custom-call(bf16[20,2560]{1,0:T(8,128)(2,1)} %bitcast.6, bf16[128,2560]{1,0:T(8,128)(2,1)} %q.1, bf16[128,512]{1,0:T(8,128)(2,1)} %k.1, bf16[128,512]{1,0:T(8,128)(2,1)} %v.1, bf16[128,2560]{1,0:T(8,128)(2,1)} %res.1, f32[2560]{0:T(1024)} %gain.1, ...), custom_call_target="tpu_custom_call" | custom-call | tf_op jit(solution)/shard_map/pallas_call | solution.py:487
  109.3 0.0 copy-start
  109.3 1.1 copy-done
  110.4 0.0 copy-start.1
  110.4 1.1 copy-done.1
  111.5 1.1 shard_map.132
Async XLA Ops:
  109.3 1.1 copy-start
  110.4 1.1 copy-start.1

commit v4 on v3

--- a/solution.py
+++ b/solution.py
@@ -20,7 +20,8 @@
 MESH = pl.DeviceIdType.MESH
 DMA = pltpu.SemaphoreType.DMA
 DELTAS = (1, 3, 2)
-PARTS = (((2, 1, 0), 0, 5), ((1, 0, 2), 5, 6), ((2, 0, 1), 11, 9))
+PARTS = (((2, 1, 0), 0, 4), ((1, 0, 2), 4, 8), ((2, 0, 1), 12, 8))
+CHUNKS = ((0, 64), (64, 64))
 KT = D // 128
 
 
@@ -46,7 +47,7 @@
 
 
 def order(i):
-    s = (i * 37) % NDEV
+    s = (i * 59) % NDEV
     return [s // 32, (s // 8) % 4, (s // 2) % 4, s % 2]
 
 
@@ -79,7 +80,7 @@
 def layer_kernel(
     w, q, k, v, res, gain, w_in, w_down, routes, gates, modal, cap, att_out, mix_out,
     G, B1, BX, Ko, Vo, Kb, Vb, qb, bias, ctx, attp, attt, normed, st, wt, win, wdn,
-    xs, xr, xf, rows, actt, pown, psend, precv, ys, ret,
+    xs, xr, xf, rows, pown, psend, precv, ys, ret,
     s1, r1, s2, r2, s3, r3, s4, r4, sb1, rb1, sb2, rb2, sb3, rb3, sb4, rb4,
     kzs, kzr, kxs, kxr, kds, kdr, cxs, cxr, ats, atr, lsem,
     dsem, drem, dloc, fsem, frem, psem, prem, ysem, yrem, yloc,
@@ -118,18 +119,18 @@
         B1[x, i] = jnp.concatenate(
             [tail[:, n * 640 + i * 128:n * 640 + i * 128 + 128] for n in range(4)], 0
         ).astype(jnp.bfloat16)
-    row = lax.broadcasted_iota(jnp.int32, (TOK, TOK), 0)
-    col = lax.broadcasted_iota(jnp.int32, (TOK, TOK), 1)
+    key_at = lax.broadcasted_iota(jnp.int32, (TOK, TOK), 0)
+    query_at = lax.broadcasted_iota(jnp.int32, (TOK, TOK), 1)
     for p in range(2):
         for j in range(9):
             ok = me - core - 8 + j + p >= 0
             if j == 0:
-                m = (col > row) & ok
+                m = (key_at > query_at) & ok
             elif j == 8:
-                m = col <= row
+                m = key_at <= query_at
             else:
-                m = (col >= 0) & ok
-            bias[p, :, j * TOK:(j + 1) * TOK] = jnp.where(m, 0.0, -jnp.inf)
+                m = (key_at >= 0) & ok
+            bias[p, j * TOK:(j + 1) * TOK] = jnp.where(m, 0.0, -jnp.inf)
     mine_q = pl.ds(pl.multiple_of(core * (D // 2), 128), D // 2)
     qb[core] = q[:, mine_q]
     for c in own:
@@ -197,12 +198,12 @@
         sl = wslice(cs, (a,), {bb: bi}, t0, tn)
         p3[pi][i] = [
             rc(G.at[sl], G.at[sl], s3.at[pi, i, n], r3.at[pi, i, n], dev(shift(cs, c, d)))
-            for n, d in enumerate(DELTAS[:2])
+            for n, d in enumerate(DELTAS[:3 if i == 3 else 2])
         ]
         if pi == 0:
             pb3[i] = [
                 rc(BX.at[y, bi], BX.at[y, bi], sb3.at[i, n], rb3.at[i, n], dev(shift(cs, 0, d)))
-                for n, d in enumerate(DELTAS[:2])
+                for n, d in enumerate(DELTAS[:3 if i == 3 else 2])
             ]
 
     p2 = [None] * 3
@@ -277,39 +278,35 @@
     cxc = []
     for hl in range(2):
         hs = slice(hl * HEAD, (hl + 1) * HEAD)
-        h = 2 * core + hl
+        first_col = (2 * core + hl) * GROUP
+        vt = jnp.transpose(Vb[:, :, hs].reshape(10 * TOK, HEAD).astype(jnp.float32)).astype(jnp.bfloat16)
         for p in range(2):
             kh = Kb[p:p + 9, :, hs].reshape(9 * TOK, HEAD)
-            vh = Vb[p:p + 9, :, hs].reshape(9 * TOK, HEAD)
+            heads = [qb[p, :, (hl * GROUP + g) * HEAD:(hl * GROUP + g + 1) * HEAD] for g in range(GROUP)]
+            st_ = lax.dot_general(
+                kh, jnp.concatenate(heads, 0), (((1,), (1,)), ((), ())), preferred_element_type=jnp.float32
+            ) * scale + jnp.concatenate([bias[p]] * GROUP, 1)
+            e = jnp.exp(st_ - jnp.max(st_, 0, keepdims=True))
+            tot = jnp.sum(e, 0, keepdims=True)
+            o = jnp.dot(
+                vt[:, p * TOK:(p + 9) * TOK], e.astype(jnp.bfloat16), preferred_element_type=jnp.float32
+            ) / tot
             for g in range(GROUP):
-                qs = slice((hl * GROUP + g) * HEAD, (hl * GROUP + g + 1) * HEAD)
-                s = lax.dot_general(
-                    qb[p, :, qs], kh, (((1,), (1,)), ((), ())), preferred_element_type=jnp.float32
-                ) * scale + bias[p]
-                mx = jnp.max(s, -1, keepdims=True)
-                e = jnp.exp(s - mx)
-                tot = jnp.sum(e, -1, keepdims=True)
-                o = jnp.dot(e.astype(jnp.bfloat16), vh, preferred_element_type=jnp.float32)
-                ctx[p, h, :, g * HEAD:(g + 1) * HEAD] = (o / tot).astype(jnp.bfloat16)
-            cxc.append(rc(ctx.at[p, h], ctx.at[p, h], cxs.at[2 * hl + p], cxr.at[2 * hl + p], sib))
-            if p == 1:
-                relay(hl + 2)
+                ctx[first_col + g, :, p * TOK:(p + 1) * TOK] = o[:, g * TOK:(g + 1) * TOK].astype(jnp.bfloat16)
+            ready = ctx.at[pl.ds(first_col, GROUP), :, pl.ds(p * TOK, TOK)]
+            cxc.append(rc(ready, ready, cxs.at[2 * hl + p], cxr.at[2 * hl + p], sib))
+            if hl == 0 and p == 0:
+                relay(2)
     for c in cxc:
         c.wait_recv()
-    for c in rl:
+    for c in rl + pb3[3] + p3[0][3] + p3[1][3] + p3[2][3]:
         c.wait_recv()
 
     def project(tile_pair):
         acc = None
         for kp in range(KT // 2):
-            lhs = tile_pair(2 * kp)
-            h, off = (2 * kp) // GROUP, (2 * kp) % GROUP
-            cols = []
-            for t in (2 * kp, 2 * kp + 1):
-                hh, oo = t // GROUP, t % GROUP
-                cols.append(ctx[:, hh, :, oo * HEAD:(oo + 1) * HEAD].reshape(2 * TOK, HEAD))
-            rhs = jnp.concatenate(cols, 1)
-            part = lax.dot_general(lhs, rhs, (((1,), (1,)), ((), ())), preferred_element_type=jnp.float32)
+            rhs = ctx[2 * kp:2 * kp + 2].reshape(2 * HEAD, 2 * TOK)
+            part = jnp.dot(tile_pair(2 * kp), rhs, preferred_element_type=jnp.float32)
             acc = part if acc is None else acc + part
         return acc.astype(jnp.bfloat16)
 
@@ -360,100 +357,73 @@
     ).reshape(NDEV, CAP, D)
     mine = pltpu.make_async_copy(xs.at[me], xr.at[0], dloc)
     mine.start()
-    HALF = NDEV // 2
 
     def offset(i, sign):
         off = order(i)
         full = [4, 4, 4, 2]
         return dev([lax.rem(cs[n] + (off[n] if sign > 0 else full[n] - off[n]), full[n]) for n in range(4)])
 
-    def send_half(half):
+    for ch, (first, size) in enumerate(CHUNKS):
+
         def send(i, c):
             t = offset(i, 1)
             pltpu.make_async_remote_copy(
-                src_ref=xs.at[t], dst_ref=xr.at[i], send_sem=dsem.at[half], recv_sem=drem.at[half],
+                src_ref=xs.at[t], dst_ref=xr.at[i], send_sem=dsem.at[ch], recv_sem=drem.at[ch],
                 device_id=(t,), device_id_type=MESH,
             ).start()
             return c
 
-        lax.fori_loop(max(1, half * HALF), (half + 1) * HALF, send, 0)
-
-    send_half(0)
-    send_half(1)
+        lax.fori_loop(max(1, first), first + size, send, 0)
     mine.wait()
 
-    def whole(src, dst, half, ss, rs):
-        n = HALF - 1 if half == 0 else HALF
-        part = pl.ds(half * HALF, n)
+    def whole(src, dst, ch, ss, rs):
+        first, size = CHUNKS[ch]
+        part = pl.ds(first, size - 1 if first == 0 else size)
         return pltpu.make_async_remote_copy(
-            src_ref=src.at[part], dst_ref=dst.at[part], send_sem=ss.at[half], recv_sem=rs.at[half],
+            src_ref=src.at[part], dst_ref=dst.at[part], send_sem=ss.at[ch], recv_sem=rs.at[ch],
             device_id=(sib,), device_id_type=MESH,
         )
 
     for c in weights:
         c.wait()
-    fwd, back = [], []
-
-    def arrive(half):
-        whole(xs, xr, half, dsem, drem).wait_recv()
-        part = pl.ds(half * HALF, HALF)
-        fwd.append(rc(xr.at[part], xf.at[part], fsem.at[half], frem.at[half], sib))
-        rows[:TOK] = xr[part].reshape(TOK, D)
-        fwd[half].wait_recv()
-        rows[TOK:] = xf[part].reshape(TOK, D)
-
-    def experts(half):
-        def hidden(n, c):
-            at = pl.ds(pl.multiple_of(n * 208, 16), 208)
-            nt = (((1,), (1,)), ((), ()))
-            gate = lax.dot_general(win[0, at], rows[...], nt, preferred_element_type=jnp.float32)
-            up = lax.dot_general(win[1, at], rows[...], nt, preferred_element_type=jnp.float32)
-            actt[at] = (gate * lax.logistic(gate) * up).astype(jnp.bfloat16)
-            return c
-
-        lax.fori_loop(0, 4, hidden, 0)
-        act = jnp.transpose(actt[...].astype(jnp.float32)).astype(jnp.bfloat16)
-        for n in range(2):
-            ls = pl.ds(n * 1280, 1280)
-            psend[half, :, ls] = jnp.dot(
-                act[TOK:], wdn[:, ls], preferred_element_type=jnp.float32
-            ).astype(jnp.bfloat16)
-        back.append(rc(psend.at[half], precv.at[half], psem.at[half], prem.at[half], sib))
-        for n in range(2):
-            ls = pl.ds(n * 1280, 1280)
-            pown[:, ls] = jnp.dot(
-                act[:TOK], wdn[:, ls], preferred_element_type=jnp.float32
-            ).astype(jnp.bfloat16)
-
-    def give(half):
-        back[half].wait_recv()
-        part = pl.ds(half * HALF, HALF)
+    nt = (((1,), (1,)), ((), ()))
+    home = pltpu.make_async_copy(ys.at[0], ret.at[me], yloc)
+    for ch, (first, size) in enumerate(CHUNKS):
+        part = pl.ds(first, size)
+        flat = pl.ds(first * CAP, size * CAP)
+        count = size * CAP
+        whole(xs, xr, ch, dsem, drem).wait_recv()
+        fwd = rc(xr.at[part], xf.at[part], fsem.at[ch], frem.at[ch], sib)
+        rows[:count] = xr[part].reshape(count, D)
+        fwd.wait_recv()
+        rows[count:2 * count] = xf[part].reshape(count, D)
+        both = rows[:2 * count]
+        gate = lax.dot_general(win[0], both, nt, preferred_element_type=jnp.float32)
+        up = lax.dot_general(win[1], both, nt, preferred_element_type=jnp.float32)
+        act = jnp.transpose(gate * lax.logistic(gate) * up).astype(jnp.bfloat16)
+        psend[flat] = jnp.dot(act[count:], wdn[...], preferred_element_type=jnp.float32).astype(jnp.bfloat16)
+        back = rc(psend.at[flat], precv.at[flat], psem.at[ch], prem.at[ch], sib)
+        pown[:count] = jnp.dot(act[:count], wdn[...], preferred_element_type=jnp.float32).astype(jnp.bfloat16)
+        back.wait_recv()
         ys[part] = (
-            pown[...].astype(jnp.float32) + precv[half].astype(jnp.float32)
-        ).astype(jnp.bfloat16).reshape(HALF, CAP, D)
-
-        def send(i, c):
+            pown[:count].astype(jnp.float32) + precv[flat].astype(jnp.float32)
+        ).astype(jnp.bfloat16).reshape(size, CAP, D)
+
+        def give(i, c):
             t = offset(i, -1)
             pltpu.make_async_remote_copy(
-                src_ref=ys.at[i], dst_ref=ret.at[me], send_sem=ysem.at[half], recv_sem=yrem.at[0],
+                src_ref=ys.at[i], dst_ref=ret.at[me], send_sem=ysem.at[ch], recv_sem=yrem.at[0],
                 device_id=(t,), device_id_type=MESH,
             ).start()
             return c
 
-        lax.fori_loop(max(1, half * HALF), (half + 1) * HALF, send, 0)
-
-    arrive(0)
-    experts(0)
-    give(0)
-    home = pltpu.make_async_copy(ys.at[0], ret.at[me], yloc)
-    home.start()
-    arrive(1)
-    experts(1)
-    give(1)
+        lax.fori_loop(max(1, first), first + size, give, 0)
+        if ch == 0:
+            home.start()
     home.wait()
-    for half in range(2):
-        whole(xs, xr, half, dsem, drem).wait_send()
-        whole(ys, ret, half, ysem, ysem).wait_send()
+    for ch in range(len(CHUNKS)):
+        whole(xs, xr, ch, dsem, drem).wait_send()
+        whole(ys, ret, ch, ysem, ysem).wait_send()
     every = pl.ds(0, NDEV - 1)
     pltpu.make_async_remote_copy(
         src_ref=ys.at[every], dst_ref=ret.at[every], send_sem=ysem.at[0], recv_sem=yrem.at[0],
@@ -498,8 +468,8 @@
             pltpu.VMEM((10, TOK, KV_HEADS * HEAD // 2), bf),
             pltpu.VMEM((10, TOK, KV_HEADS * HEAD // 2), bf),
             pltpu.VMEM((2, TOK, D // 2), bf),
-            pltpu.VMEM((2, TOK, 9 * TOK), jnp.float32),
-            pltpu.VMEM((2, KV_HEADS, TOK, GROUP * HEAD), bf),
+            pltpu.VMEM((2, 9 * TOK, TOK), jnp.float32),
+            pltpu.VMEM((KT, HEAD, 2 * TOK), bf),
             pltpu.VMEM((2, 2, 1280, TOK), bf),
             pltpu.VMEM((D, TOK), jnp.float32),
             pltpu.VMEM((TOK, D), bf),
@@ -511,19 +481,18 @@
             pltpu.VMEM((NDEV, CAP, D), bf),
             pltpu.VMEM((NDEV, CAP, D), bf),
             pltpu.VMEM((2 * TOK, D), bf),
-            pltpu.VMEM((cols, 2 * TOK), bf),
             pltpu.VMEM((TOK, D), bf),
-            pltpu.VMEM((2, TOK, D), bf),
-            pltpu.VMEM((2, TOK, D), bf),
+            pltpu.VMEM((2 * TOK, D), bf),
+            pltpu.VMEM((2 * TOK, D), bf),
             pltpu.VMEM((NDEV, CAP, D), bf),
             pltpu.VMEM((NDEV, CAP, D), bf),
             DMA((3, 3)), DMA((3, 3)), DMA((3, 3)), DMA((3, 3)),
-            DMA((3, 4, 2)), DMA((3, 4, 2)), DMA((3, 4, 2)), DMA((3, 4, 2)),
+            DMA((3, 4, 3)), DMA((3, 4, 3)), DMA((3, 4, 2)), DMA((3, 4, 2)),
             DMA((3,)), DMA((3,)), DMA((3,)), DMA((3,)),
-            DMA((4, 2)), DMA((4, 2)), DMA((4, 2)), DMA((4, 2)),
+            DMA((4, 3)), DMA((4, 3)), DMA((4, 2)), DMA((4, 2)),
             DMA((2, 2)), DMA((2, 2)), DMA((2, 3, 2)), DMA((2, 3, 2)), DMA((2,)), DMA((2,)),
             DMA((5,)), DMA((5,)), DMA, DMA, DMA((8,)),
-            DMA((2,)), DMA((2,)), DMA, DMA((2,)), DMA((2,)), DMA((2,)), DMA((2,)), DMA((2,)), DMA((1,)), DMA,
+            DMA((3,)), DMA((3,)), DMA, DMA((3,)), DMA((3,)), DMA((3,)), DMA((3,)), DMA((3,)), DMA((1,)), DMA,
         ],
         compiler_params=pltpu.CompilerParams(
             has_side_effects=True, collective_id=0, vmem_limit_bytes=60 * 2**20

time: 113 us -> 107 us (0.947)
  Pallas kernels: 110 us -> 104 us
    pallas_call x1, Pallas kernels: 109 us -> 103 us  [body(): pl.pallas_call(layer_kernel, out_shape=(jax.ShapeDtypeStruct((TOK, D), bf...]
where the time goes in v4:
time: 107 us
  Pallas kernels  104 us (97%)
  local copies, waits for them, and re-layouts  2.17 us (2%)
    pallas_call x1, Pallas kernels, body(): pl.pallas_call(layer_kernel, out_shape=(jax.ShapeDtypeStruct((TOK, D), bf...  103 us
    unnamed x4, local copies, waits for them, and re-layouts  2.17 us

profile of v4, /device:TPU:1, one launch (start us, length us, event | category | flops | bytes accessed | tf_op | source)
XLA Modules:
  0.0 107.2 jit_solution(4197200239770120364)
XLA Ops:
  0.6 103.2 %shard_map.131 = (bf16[128,2560]{1,0:T(8,128)(2,1)}, bf16[128,2560]{1,0:T(8,128)(2,1)}) custom-call(bf16[20,2560]{1,0:T(8,128)(2,1)} %bitcast.6, bf16[128,2560]{1,0:T(8,128)(2,1)} %q.1, bf16[128,512]{1,0:T(8,128)(2,1)} %k.1, bf16[128,512]{1,0:T(8,128)(2,1)} %v.1, bf16[128,2560]{1,0:T(8,128)(2,1)} %res.1, f32[2560]{0:T(1024)} %gain.1, ...), custom_call_target="tpu_custom_call" | custom-call | tf_op jit(solution)/shard_map/pallas_call | solution.py:457
  103.8 0.0 copy-start
  103.8 1.1 %copy-done = bf16[128,2560]{1,0:T(8,128)(2,1)S(1)} copy-done((bf16[128,2560]{1,0:T(8,128)(2,1)S(1)}, bf16[128,2560]{1,0:T(8,128)(2,1)}, u32[]{:S(2)}) %copy-start) | copy-done | bytes 655384
  104.9 0.0 copy-start.1
  104.9 1.1 %copy-done.1 = bf16[128,2560]{1,0:T(8,128)(2,1)S(1)} copy-done((bf16[128,2560]{1,0:T(8,128)(2,1)S(1)}, bf16[128,2560]{1,0:T(8,128)(2,1)}, u32[]{:S(2)}) %copy-start.1) | copy-done | bytes 655384
  106.0 1.1 shard_map.132
Async XLA Ops:
  103.8 1.1 %copy-start = (bf16[128,2560]{1,0:T(8,128)(2,1)S(1)}, bf16[128,2560]{1,0:T(8,128)(2,1)}, u32[]{:S(2)}) copy-start(bf16[128,2560]{1,0:T(8,128)(2,1)} %get-tuple-element.4.a) | copy-start | bytes 1966084
  104.9 1.1 %copy-start.1 = (bf16[128,2560]{1,0:T(8,128)(2,1)S(1)}, bf16[128,2560]{1,0:T(8,128)(2,1)}, u32[]{:S(2)}) copy-start(bf16[128,2560]{1,0:T(8,128)(2,1)} %get-tuple-element.5.b) | copy-start | bytes 1966084

commit v5 on v4

--- a/solution.py
+++ b/solution.py
@@ -51,10 +51,20 @@
     return [s // 32, (s // 8) % 4, (s // 2) % 4, s % 2]
 
 
-def routing(routes, gates, modal, cap, st, wt):
+def routing(cs, routes, gates, modal, cap, st, wt):
     rows = 2 * NDEV
     rho = lax.broadcasted_iota(jnp.int32, (rows, TOK), 0)
-    key, turn = jnp.right_shift(rho, 1), jnp.bitwise_and(rho, 1)
+    turn = jnp.bitwise_and(rho, 1)
+
+    def device(at):
+        off = jnp.bitwise_and(jnp.right_shift(at, 1) * 59, NDEV - 1)
+        y, z, x, core = cs
+        ny = jnp.bitwise_and(y + jnp.right_shift(off, 5), 3)
+        nz = jnp.bitwise_and(z + jnp.bitwise_and(jnp.right_shift(off, 3), 3), 3)
+        nx = jnp.bitwise_and(x + jnp.bitwise_and(jnp.right_shift(off, 1), 3), 3)
+        return ny * 32 + nz * 8 + nx * 2 + jnp.bitwise_and(core + off, 1)
+
+    key = device(rho)
     mod = modal[...][None, :]
     is0 = key == routes[0:1] * 2 + mod
     is1 = key == routes[1:2] * 2 + mod
@@ -64,9 +74,9 @@
         hit.astype(jnp.bfloat16), jnp.where(before, 1.0, 0.0).astype(jnp.bfloat16),
         preferred_element_type=jnp.float32,
     )
-    rho_e = lax.broadcasted_iota(jnp.int32, (rows, EXPERTS), 0)
-    at_e = lax.broadcasted_iota(jnp.int32, (rows, EXPERTS), 1) == jnp.right_shift(rho_e, 2)
-    cap_e = jnp.where(jnp.bitwise_and(rho_e, 2) == 0, cap[0:1], cap[1:2]).astype(jnp.float32)
+    key_e = device(lax.broadcasted_iota(jnp.int32, (rows, EXPERTS), 0))
+    at_e = lax.broadcasted_iota(jnp.int32, (rows, EXPERTS), 1) == jnp.right_shift(key_e, 1)
+    cap_e = jnp.where(jnp.bitwise_and(key_e, 1) == 0, cap[0:1], cap[1:2]).astype(jnp.float32)
     limit = jnp.sum(jnp.where(at_e, cap_e, 0.0), -1, keepdims=True)
     turn_f = turn.astype(jnp.float32)
     kept = jnp.where((rank == turn_f) & (turn_f < limit), hit, 0.0)
@@ -268,7 +278,7 @@
                     rl.append(rc(b_, b_, sb4.at[i, n], rb4.at[i, n], dev(shift(cs, 0, dto))))
 
     relay(0)
-    routing(routes, gates, modal, cap, st, wt)
+    routing(cs, routes, gates, modal, cap, st, wt)
     relay(1)
     for c in kvd + kvx_wait:
         c.wait_recv()
@@ -352,28 +362,33 @@
         hd = res[:, ls].astype(jnp.float32) + att_out[:, ls].astype(jnp.float32)
         normed[:, ls] = (hd * inv * gain[ls][None, :]).astype(jnp.bfloat16)
 
-    xs[...] = jnp.dot(st[...], normed[...], preferred_element_type=jnp.float32).astype(
-        jnp.bfloat16
-    ).reshape(NDEV, CAP, D)
-    mine = pltpu.make_async_copy(xs.at[me], xr.at[0], dloc)
-    mine.start()
 
     def offset(i, sign):
         off = order(i)
         full = [4, 4, 4, 2]
         return dev([lax.rem(cs[n] + (off[n] if sign > 0 else full[n] - off[n]), full[n]) for n in range(4)])
 
-    for ch, (first, size) in enumerate(CHUNKS):
-
-        def send(i, c):
-            t = offset(i, 1)
-            pltpu.make_async_remote_copy(
-                src_ref=xs.at[t], dst_ref=xr.at[i], send_sem=dsem.at[ch], recv_sem=drem.at[ch],
-                device_id=(t,), device_id_type=MESH,
-            ).start()
-            return c
-
-        lax.fori_loop(max(1, first), first + size, send, 0)
+    mine = pltpu.make_async_copy(xs.at[0], xr.at[0], dloc)
+    for piece in range(2):
+        part = slice(piece * NDEV // 2, (piece + 1) * NDEV // 2)
+        xs[part] = jnp.dot(
+            st[piece * NDEV:(piece + 1) * NDEV], normed[...], preferred_element_type=jnp.float32
+        ).astype(jnp.bfloat16).reshape(NDEV // 2, CAP, D)
+        if piece == 0:
+            mine.start()
+        for ch, (first, size) in enumerate(CHUNKS):
+
+            def send(i, c):
+                t = offset(i, 1)
+                pltpu.make_async_remote_copy(
+                    src_ref=xs.at[i], dst_ref=xr.at[i], send_sem=dsem.at[ch], recv_sem=drem.at[ch],
+                    device_id=(t,), device_id_type=MESH,
+                ).start()
+                return c
+
+            low, high = max(1, first, part.start), min(first + size, part.stop)
+            if low < high:
+                lax.fori_loop(low, high, send, 0)
     mine.wait()
 
     def whole(src, dst, ch, ss, rs):
@@ -387,14 +402,39 @@
     for c in weights:
         c.wait()
     nt = (((1,), (1,)), ((), ()))
-    home = pltpu.make_async_copy(ys.at[0], ret.at[me], yloc)
+    home = pltpu.make_async_copy(ys.at[0], ret.at[0], yloc)
+    backs = []
+
+    def give_back(ch):
+        first, size = CHUNKS[ch]
+        count = size * CAP
+        flat = pl.ds(first * CAP, count)
+        backs[ch].wait_recv()
+        ys[first:first + size] = (
+            pown[:count].astype(jnp.float32) + precv[flat].astype(jnp.float32)
+        ).astype(jnp.bfloat16).reshape(size, CAP, D)
+
+        def give(i, c):
+            t = offset(i, -1)
+            pltpu.make_async_remote_copy(
+                src_ref=ys.at[i], dst_ref=ret.at[i], send_sem=ysem.at[ch], recv_sem=yrem.at[0],
+                device_id=(t,), device_id_type=MESH,
+            ).start()
+            return c
+
+        lax.fori_loop(max(1, first), first + size, give, 0)
+        if ch == 0:
+            home.start()
+
     for ch, (first, size) in enumerate(CHUNKS):
         part = pl.ds(first, size)
-        flat = pl.ds(first * CAP, size * CAP)
         count = size * CAP
+        flat = pl.ds(first * CAP, count)
         whole(xs, xr, ch, dsem, drem).wait_recv()
         fwd = rc(xr.at[part], xf.at[part], fsem.at[ch], frem.at[ch], sib)
         rows[:count] = xr[part].reshape(count, D)
+        if ch > 0:
+            give_back(ch - 1)
         fwd.wait_recv()
         rows[count:2 * count] = xf[part].reshape(count, D)
         both = rows[:2 * count]
@@ -402,24 +442,9 @@
         up = lax.dot_general(win[1], both, nt, preferred_element_type=jnp.float32)
         act = jnp.transpose(gate * lax.logistic(gate) * up).astype(jnp.bfloat16)
         psend[flat] = jnp.dot(act[count:], wdn[...], preferred_element_type=jnp.float32).astype(jnp.bfloat16)
-        back = rc(psend.at[flat], precv.at[flat], psem.at[ch], prem.at[ch], sib)
+        backs.append(rc(psend.at[flat], precv.at[flat], psem.at[ch], prem.at[ch], sib))
         pown[:count] = jnp.dot(act[:count], wdn[...], preferred_element_type=jnp.float32).astype(jnp.bfloat16)
-        back.wait_recv()
-        ys[part] = (
-            pown[:count].astype(jnp.float32) + precv[flat].astype(jnp.float32)
-        ).astype(jnp.bfloat16).reshape(size, CAP, D)
-
-        def give(i, c):
-            t = offset(i, -1)
-            pltpu.make_async_remote_copy(
-                src_ref=ys.at[i], dst_ref=ret.at[me], send_sem=ysem.at[ch], recv_sem=yrem.at[0],
-                device_id=(t,), device_id_type=MESH,
-            ).start()
-            return c
-
-        lax.fori_loop(max(1, first), first + size, give, 0)
-        if ch == 0:
-            home.start()
+    give_back(len(CHUNKS) - 1)
     home.wait()
     for ch in range(len(CHUNKS)):
         whole(xs, xr, ch, dsem, drem).wait_send()
@@ -492,7 +517,7 @@
             DMA((4, 3)), DMA((4, 3)), DMA((4, 2)), DMA((4, 2)),
             DMA((2, 2)), DMA((2, 2)), DMA((2, 3, 2)), DMA((2, 3, 2)), DMA((2,)), DMA((2,)),
             DMA((5,)), DMA((5,)), DMA, DMA, DMA((8,)),
-            DMA((3,)), DMA((3,)), DMA, DMA((3,)), DMA((3,)), DMA((3,)), DMA((3,)), DMA((3,)), DMA((1,)), DMA,
+            DMA((4,)), DMA((4,)), DMA, DMA((4,)), DMA((4,)), DMA((4,)), DMA((4,)), DMA((4,)), DMA((1,)), DMA,
         ],
         compiler_params=pltpu.CompilerParams(
             has_side_effects=True, collective_id=0, vmem_limit_bytes=60 * 2**20

time: 107 us -> 105 us (0.981)
  Pallas kernels: 104 us -> 102 us
    pallas_call x1, Pallas kernels: 103 us -> 101 us  [body(): pl.pallas_call(layer_kernel, out_shape=(jax.ShapeDtypeStruct((TOK, D), bf...]
where the time goes in v5:
time: 105 us
  Pallas kernels  102 us (97%)
  local copies, waits for them, and re-layouts  2.17 us (2%)
    pallas_call x1, Pallas kernels, body(): pl.pallas_call(layer_kernel, out_shape=(jax.ShapeDtypeStruct((TOK, D), bf...  101 us
    unnamed x4, local copies, waits for them, and re-layouts  2.17 us

profile of v5, /device:TPU:1, one launch (start us, length us, event | category | flops | bytes accessed | tf_op | source)
XLA Modules:
  0.0 105.2 jit_solution(16989024277052398377)
XLA Ops:
  0.6 101.2 %shard_map.131 = (bf16[128,2560]{1,0:T(8,128)(2,1)}, bf16[128,2560]{1,0:T(8,128)(2,1)}) custom-call(bf16[20,2560]{1,0:T(8,128)(2,1)} %bitcast.6, bf16[128,2560]{1,0:T(8,128)(2,1)} %q.1, bf16[128,512]{1,0:T(8,128)(2,1)} %k.1, bf16[128,512]{1,0:T(8,128)(2,1)} %v.1, bf16[128,2560]{1,0:T(8,128)(2,1)} %res.1, f32[2560]{0:T(1024)} %gain.1, ...), custom_call_target="tpu_custom_call" | custom-call | tf_op jit(solution)/shard_map/pallas_call | solution.py:482
  101.8 0.0 copy-start
  101.8 1.1 %copy-done = bf16[128,2560]{1,0:T(8,128)(2,1)S(1)} copy-done((bf16[128,2560]{1,0:T(8,128)(2,1)S(1)}, bf16[128,2560]{1,0:T(8,128)(2,1)}, u32[]{:S(2)}) %copy-start) | copy-done | bytes 655384
  102.9 0.0 copy-start.1
  102.9 1.1 %copy-done.1 = bf16[128,2560]{1,0:T(8,128)(2,1)S(1)} copy-done((bf16[128,2560]{1,0:T(8,128)(2,1)S(1)}, bf16[128,2560]{1,0:T(8,128)(2,1)}, u32[]{:S(2)}) %copy-start.1) | copy-done | bytes 655384
  104.0 1.1 %shard_map.132 = (bf16[128,2560]{1,0:T(8,128)(2,1)}, bf16[128,2560]{1,0:T(8,128)(2,1)}) custom-call(bf16[128,2560]{1,0:T(8,128)(2,1)S(1)} %copy-done, bf16[128,2560]{1,0:T(8,128)(2,1)S(1)} %copy-done.1), custom_call_target="tpu_custom_call" | custom-call | tf_op jit(solution)/shard_map/pallas_call | solution.py:530
Async XLA Ops:
  101.8 1.1 %copy-start = (bf16[128,2560]{1,0:T(8,128)(2,1)S(1)}, bf16[128,2560]{1,0:T(8,128)(2,1)}, u32[]{:S(2)}) copy-start(bf16[128,2560]{1,0:T(8,128)(2,1)} %get-tuple-element.4.a) | copy-start | bytes 1966084
  102.9 1.1 %copy-start.1 = (bf16[128,2560]{1,0:T(8,128)(2,1)S(1)}, bf16[128,2560]{1,0:T(8,128)(2,1)}, u32[]{:S(2)}) copy-start(bf16[128,2560]{1,0:T(8,128)(2,1)} %get-tuple-element.5.b) | copy-start | bytes 1966084

commit v6 on v5

--- a/solution.py
+++ b/solution.py
@@ -88,7 +88,7 @@
 
 
 def layer_kernel(
-    w, q, k, v, res, gain, w_in, w_down, routes, gates, modal, cap, att_out, mix_out,
+    w, q, k, v, res, gain, w_in, w_down, routes, gates, modal, cap, att_out, mix_out, att_v, att_sem,
     G, B1, BX, Ko, Vo, Kb, Vb, qb, bias, ctx, attp, attt, normed, st, wt, win, wdn,
     xs, xr, xf, rows, pown, psend, precv, ys, ret,
     s1, r1, s2, r2, s3, r3, s4, r4, sb1, rb1, sb2, rb2, sb3, rb3, sb4, rb4,
@@ -305,7 +305,7 @@
                 ctx[first_col + g, :, p * TOK:(p + 1) * TOK] = o[:, g * TOK:(g + 1) * TOK].astype(jnp.bfloat16)
             ready = ctx.at[pl.ds(first_col, GROUP), :, pl.ds(p * TOK, TOK)]
             cxc.append(rc(ready, ready, cxs.at[2 * hl + p], cxr.at[2 * hl + p], sib))
-            if hl == 0 and p == 0:
+            if hl == 0 and p == 1:
                 relay(2)
     for c in cxc:
         c.wait_recv()
@@ -353,15 +353,16 @@
     for t in range(KT):
         ls = slice(t * 128, (t + 1) * 128)
         a_ = jnp.transpose(attt[ls])
-        att_out[:, ls] = a_.astype(jnp.bfloat16)
+        att_v[:, ls] = a_.astype(jnp.bfloat16)
         hd = res[:, ls].astype(jnp.float32) + a_
         ssq = ssq + jnp.sum(hd * hd, -1, keepdims=True)
     inv = lax.rsqrt(ssq / D + 1e-05)
     for t in range(KT):
         ls = slice(t * 128, (t + 1) * 128)
-        hd = res[:, ls].astype(jnp.float32) + att_out[:, ls].astype(jnp.float32)
+        hd = res[:, ls].astype(jnp.float32) + att_v[:, ls].astype(jnp.float32)
         normed[:, ls] = (hd * inv * gain[ls][None, :]).astype(jnp.bfloat16)
 
+    early = pltpu.make_async_copy(att_v, att_out, att_sem)
 
     def offset(i, sign):
         off = order(i)
@@ -390,6 +391,7 @@
             if low < high:
                 lax.fori_loop(low, high, send, 0)
     mine.wait()
+    early.start()
 
     def whole(src, dst, ch, ss, rs):
         first, size = CHUNKS[ch]
@@ -459,16 +461,25 @@
         wt[1], back_rows, preferred_element_type=jnp.float32
     )
     mix_out[...] = (mix * (1.0 / 1024.0)).astype(jnp.bfloat16)
+    early.wait()
     for c in sends:
         c.wait_send()
 
 
-def out_kernel(a, b, a_out, b_out, sem):
-    copies = [pltpu.make_async_copy(a, a_out, sem.at[0]), pltpu.make_async_copy(b, b_out, sem.at[1])]
-    for c in copies:
+def out_kernel(a, b, a_out, b_out, a_buf, b_buf, sem_in, sem_out):
+    loads, stores = [], []
+    for n, (src, buf, dst) in enumerate(((a, a_buf, a_out), (b, b_buf, b_out))):
+        for h in range(2):
+            part = pl.ds(h * TOK // 2, TOK // 2)
+            loads.append(pltpu.make_async_copy(src.at[part], buf.at[part], sem_in.at[n, h]))
+            stores.append(pltpu.make_async_copy(buf.at[part], dst.at[part], sem_out.at[n, h]))
+    for c in loads:
         c.start()
-    for c in copies:
+    for c, d in zip(loads, stores):
         c.wait()
+        d.start()
+    for d in stores:
+        d.wait()
 
 
 def body(
@@ -483,8 +494,10 @@
         layer_kernel,
         out_shape=(jax.ShapeDtypeStruct((TOK, D), bf), jax.ShapeDtypeStruct((TOK, D), bf)),
         in_specs=[vm, vm, any_, any_, vm, vm, any_, any_, vm, vm, vm, vm],
-        out_specs=(vm, vm),
+        out_specs=(any_, vm),
         scratch_shapes=[
+            pltpu.VMEM((TOK, D), bf),
+            DMA,
             pltpu.VMEM((4, 4, 4, KT, 16, 128), bf),
             pltpu.VMEM((4, 5, 16, 128), bf),
             pltpu.VMEM((4, 4, KT, 16, 128), bf),
@@ -528,8 +541,12 @@
     )
     shape = jax.ShapeDtypeStruct((TOK, D), bf)
     return pl.pallas_call(
-        out_kernel, out_shape=(shape, shape), in_specs=[vm, vm], out_specs=(any_, any_), scratch_shapes=[DMA((2,))],
-        compiler_params=pltpu.CompilerParams(vmem_limit_bytes=4 * 2**20),
+        out_kernel,
+        out_shape=(shape, shape),
+        in_specs=[any_, any_],
+        out_specs=(any_, any_),
+        scratch_shapes=[pltpu.VMEM((TOK, D), bf), pltpu.VMEM((TOK, D), bf), DMA((2, 2)), DMA((2, 2))],
+        compiler_params=pltpu.CompilerParams(vmem_limit_bytes=60 * 2**20),
     )(*outs)
 
 

time: 105 us -> 102 us (0.971)
  local copies, waits for them, and re-layouts: 2.17 us -> 0 us
    unnamed x4 -> x0, local copies, waits for them, and re-layouts: 2.17 us -> none
    pallas_call x1, Pallas kernels: 101 us -> 99.2 us  [body(): pl.pallas_call(layer_kernel, out_shape=(jax.ShapeDtypeStruct((TOK, D), bf...]
where the time goes in v6:
time: 102 us
  Pallas kernels  101 us (99%)
    pallas_call x1, Pallas kernels, body(): pl.pallas_call(layer_kernel, out_shape=(jax.ShapeDtypeStruct((TOK, D), bf...  99.2 us
    pallas_call x1, Pallas kernels, body(): pl.pallas_call(out_kernel, out_shape=(shape, shape), in_specs=[any_, any_...  2.09 us

profile of v6, /device:TPU:1, one launch (start us, length us, event | category | flops | bytes accessed | tf_op | source)
XLA Modules:
  0.0 102.0 jit_solution(14868523012883450494)
XLA Ops:
  0.6 99.2 %shard_map.131 = (bf16[128,2560]{1,0:T(8,128)(2,1)}, bf16[128,2560]{1,0:T(8,128)(2,1)}) custom-call(bf16[20,2560]{1,0:T(8,128)(2,1)} %bitcast.6, bf16[128,2560]{1,0:T(8,128)(2,1)} %q.1, bf16[128,512]{1,0:T(8,128)(2,1)} %k.1, bf16[128,512]{1,0:T(8,128)(2,1)} %v.1, bf16[128,2560]{1,0:T(8,128)(2,1)} %res.1, f32[2560]{0:T(1024)} %gain.1, ...), custom_call_target="tpu_custom_call" | custom-call | tf_op jit(solution)/shard_map/pallas_call | solution.py:493
  99.8 2.1 %shard_map.132 = (bf16[128,2560]{1,0:T(8,128)(2,1)}, bf16[128,2560]{1,0:T(8,128)(2,1)}) custom-call(bf16[128,2560]{1,0:T(8,128)(2,1)} %get-tuple-element.4.a, bf16[128,2560]{1,0:T(8,128)(2,1)} %get-tuple-element.5.b), custom_call_target="tpu_custom_call" | custom-call | tf_op jit(solution)/shard_map/pallas_call | solution.py:543
